TPU v7x, 32 devices: a whole 2x2x4 slice. The times are simulated.
32 devices in a mesh: fluid: 8 (over y, x, core), solid: 4 (over z).
Axes of the slice: x: 2, y: 2, z: 4, core: 2. Of those that a mesh axis runs over, the one named last changes fastest.
Arguments:
- rbf_blocks: bfloat16 [3328, 256, 256], P(('fluid', 'solid')), may hold values from -0.375 to 0.375
- fluid_traction: bfloat16 [3328, 768], P(('fluid', 'solid')), may hold values from -24 to 24
- fluid_mass: bfloat16 [3328, 768], P(('fluid', 'solid')), may hold values from 0.19921875 to 2
- route: int32 [3328, 1], P(('fluid', 'solid')), may hold values from 0 to 31; in each aligned block of 104 rows (0 to 103, 104 to 207, ...) at most 6 rows name the same one
- slot: int32 [3328], P(('fluid', 'solid')), may hold values from 0 to 7
- shell_inverse: bfloat16 [256, 768, 768], P(('fluid', 'solid')), may hold values from -0.0078125 to 0.0078125
- robin_coef: float32 [256, 768], P(('fluid', 'solid')), may hold values from 1 to 27
- shell_start: float32 [256, 768], P(('fluid', 'solid')), may hold values from -3 to 3
Outputs:
- shell_displacement: float32 [256, 768], P(('fluid', 'solid'))
- fluid_load: bfloat16 [3328, 768], P(('fluid', 'solid'))
- residual_norms: float32 [6], replicated
Inputs may be any that keep to these rules, and one draw needn't show every extreme that they name: `route`: among the 104 blocks of one device at most 6 name the same owner device.
All inputs are finite; a program needn't handle non-finite values.
Results may differ from a plain program's by a relative error of at most 0.009.
Values may be sent and summed in bfloat16 or wider, within the bound.
A program may use at most 128 MiB of HBM per device.

v0:
```python
import functools

import jax
import jax.numpy as jnp
from jax import lax
from jax.experimental import pallas as pl
from jax.experimental.pallas import tpu as pltpu
from jax.sharding import PartitionSpec as P

ITERS = 6


RELAX = 0.3
EPSILON = 1e-06


def transport(buffer, devices, capacity):
    breadth = buffer.shape[1]
    moved = lax.all_to_all(
        buffer.reshape(devices, capacity, breadth),
        ("fluid", "solid"),
        split_axis=0,
        concat_axis=0,
        tiled=True,
    )
    return moved.reshape(devices * capacity, breadth)


def least_squares(gram, target_side):
    order = gram.shape[0]
    lower = [[None] * order for _ in range(order)]
    for row in range(order):
        for column in range(row + 1):
            total = gram[row, column]
            for inner in range(column):
                total = total - lower[row][inner] * lower[column][inner]
            if row == column:
                lower[row][row] = jnp.sqrt(total)
            else:
                lower[row][column] = total / lower[column][column]
    middle = []
    for row in range(order):
        total = target_side[row]
        for inner in range(row):
            total = total - lower[row][inner] * middle[inner]
        middle.append(total / lower[row][row])
    result = [None] * order
    for row in reversed(range(order)):
        total = middle[row]
        for inner in range(row + 1, order):
            total = total - lower[inner][row] * result[inner]
        result[row] = total / lower[row][row]
    return jnp.stack(result)


def per_device(
    rbf_blocks, fluid_traction, fluid_mass, route, slot, shell_inverse, robin_coef, shell_start
):
    devices = lax.axis_size("fluid") * lax.axis_size("solid")
    blocks = rbf_blocks.shape[0]
    nodes = rbf_blocks.shape[1]
    breadth = 3 * nodes
    shells = shell_inverse.shape[0]
    capacity = max(2, 2 * blocks // devices)
    slots_all = devices * capacity
    destination = route[:, 0]
    block_order = jnp.arange(blocks, dtype=jnp.int32)
    earlier = (destination[:, None] == destination[None, :]) & (
        block_order[None, :] < block_order[:, None]
    )
    slot_rank = jnp.sum(earlier.astype(jnp.int32), axis=1)
    position = destination * capacity + slot_rank
    positions = jnp.arange(slots_all, dtype=jnp.int32)
    placing = positions[:, None] == position[None, :]
    place_out = placing.astype(jnp.bfloat16)
    place_in = (position[:, None] == positions[None, :]).astype(jnp.bfloat16)
    wanted = jnp.max(jnp.where(placing, slot[None, :] + 1, 0), axis=1) - 1
    asked = lax.all_to_all(
        wanted.reshape(devices, capacity),
        ("fluid", "solid"),
        split_axis=0,
        concat_axis=0,
        tiled=True,
    ).reshape(slots_all)
    shell_ids = jnp.arange(shells, dtype=jnp.int32)
    picking = (asked[:, None] == shell_ids[None, :]).astype(jnp.bfloat16)
    collecting = (shell_ids[:, None] == asked[None, :]).astype(jnp.bfloat16)
    traction = fluid_traction.astype(jnp.float32)
    massive = fluid_mass.astype(jnp.float32)
    count = shells * devices * breadth
    current = shell_start
    residuals = []
    images = []
    norms = []
    last_load = None
    for iteration in range(ITERS):
        current_half = current.astype(jnp.bfloat16)
        outgoing = jnp.dot(picking, current_half, preferred_element_type=jnp.float32).astype(
            jnp.bfloat16
        )
        incoming = transport(outgoing, devices, capacity)
        displaced = jnp.dot(place_in, incoming, preferred_element_type=jnp.float32).astype(
            jnp.bfloat16
        )
        moved = jnp.einsum(
            "bcj,bij->bci",
            displaced.reshape(blocks, 3, nodes),
            rbf_blocks,
            preferred_element_type=jnp.float32,
        ).reshape(blocks, breadth)
        load = (traction - massive * moved).astype(jnp.bfloat16)
        last_load = load
        mapped = (
            jnp.einsum(
                "bci,bij->bcj",
                load.reshape(blocks, 3, nodes),
                rbf_blocks,
                preferred_element_type=jnp.float32,
            )
            .reshape(blocks, breadth)
            .astype(jnp.bfloat16)
        )
        sending = jnp.dot(place_out, mapped, preferred_element_type=jnp.float32).astype(
            jnp.bfloat16
        )
        arrived = transport(sending, devices, capacity)
        shell_load = jnp.dot(collecting, arrived, preferred_element_type=jnp.float32)
        forcing = (shell_load + robin_coef * current).astype(jnp.bfloat16)
        image = jnp.einsum("bi,bij->bj", forcing, shell_inverse, preferred_element_type=jnp.float32)
        residual = image - current
        residuals.append(residual)
        images.append(image)
        squares_local = jnp.sum(residual * residual)
        if iteration == 0:
            gram_local = jnp.zeros((1, 1), jnp.float32)
            rhs_local = jnp.zeros((1,), jnp.float32)
        else:
            changes = jnp.stack(
                [(residuals[i + 1] - residuals[i]).reshape(-1) for i in range(iteration)]
            )
            gram_local = jnp.dot(changes, changes.T, precision=lax.Precision.HIGHEST)
            rhs_local = jnp.dot(changes, residual.reshape(-1), precision=lax.Precision.HIGHEST)
        gram, rhs, squares = lax.psum((gram_local, rhs_local, squares_local), ("fluid", "solid"))
        norms.append(jnp.sqrt(squares / count + EPSILON))
        if iteration == 0:
            current = current + RELAX * residual
        else:
            image_changes = jnp.stack([images[i + 1] - images[i] for i in range(iteration)])
            coefs = least_squares(gram, -rhs)
            current = image + jnp.tensordot(
                coefs, image_changes, axes=1, precision=lax.Precision.HIGHEST
            )
    return (current, last_load, jnp.stack(norms))


CHUNK = 26
LANES = 128
VMEM_BYTES = 67043328
MESH = pl.DeviceIdType.MESH


def kernel(
    nf, nz, blocks, nodes, shells, count,
    key_ref, row_ref, tr_ref, ms_ref, robin_ref, start_ref, rbf_hbm, inv_hbm,
    cur_out, load_out, norm_out,
    rbf, inv, slots, curb, cur_own, vhist, rprev, sc, place, collect, disp, loadf, mapped,
    part, send_a, recv_a, send_b, recv_b, send_c, recv_c, shell_sum,
    rbf_sem, inv_sem,
    s1, r1, s2, r2, s3, r3, sa, ra, sb, rb, sc_s, sc_r,
):
    f32, bf16 = jnp.float32, jnp.bfloat16
    breadth = 3 * nodes
    nxy = nf // 2
    group = nz * shells
    every = nf * group
    f = lax.axis_index("fluid")
    z = lax.axis_index("solid")
    xy = f // 2
    core = lax.rem(f, 2)
    other = 1 - core
    nchunk = blocks // CHUNK
    rows = disp.shape[0]

    def turn(value, step, size):
        return lax.rem(value + step + size, size)

    def fluid_of(plane, unit):
        return plane * 2 + unit

    def first_row(plane, unit, depth):
        return pl.multiple_of((fluid_of(plane, unit) * nz + depth) * shells, shells)

    def rbf_copy(i):
        at = pl.ds(i * CHUNK, CHUNK)
        return pltpu.make_async_copy(rbf_hbm.at[at], rbf.at[at], rbf_sem.at[i])

    def inv_copy():
        return pltpu.make_async_copy(inv_hbm, inv, inv_sem)

    def start_rbf(i, carry):
        rbf_copy(i).start()
        return carry

    lax.fori_loop(0, nchunk, start_rbf, 0)
    inv_copy().start()

    own_row = first_row(xy, core, z)
    for j in range(ITERS + 1):
        slots[j] = jnp.zeros(slots.shape[1:], f32)
    slots[0, pl.ds(own_row, shells), 0:breadth] = start_ref[...]
    vhist[...] = jnp.zeros(vhist.shape, f32)
    sc[...] = jnp.zeros(sc.shape, f32)
    rprev[...] = jnp.zeros(rprev.shape, f32)
    mapped[...] = jnp.zeros(mapped.shape, f32)
    loadf[...] = jnp.zeros(loadf.shape, f32)

    barrier = pltpu.get_barrier_semaphore()
    for d in range(1, nz):
        pl.semaphore_signal(barrier, inc=1, device_id=(f, turn(z, d, nz)), device_id_type=MESH)
    for e in range(1, nxy):
        pl.semaphore_signal(
            barrier, inc=1, device_id=(fluid_of(turn(xy, e, nxy), core), z), device_id_type=MESH
        )
    pl.semaphore_signal(barrier, inc=1, device_id=(fluid_of(xy, other), z), device_id_type=MESH)

    place[...] = jnp.where(
        key_ref[...] == lax.broadcasted_iota(jnp.int32, (rows, 3 * every), 1), 1.0, 0.0
    ).astype(bf16)
    for side in range(2):
        unit = core if side == 0 else other
        line = lax.broadcasted_iota(jnp.int32, (nxy * group, 1), 0)
        ids = (line // group * 2 + unit) * group + lax.rem(line, group)
        for c in range(3):
            collect[side, c] = jnp.where(ids + c * every == row_ref[...], 1.0, 0.0).astype(bf16)

    pl.semaphore_wait(barrier, (nz - 1) + (nxy - 1) + 1)

    def all_gather(j, lanes):
        def block(plane, unit, depth):
            return slots.at[j, pl.ds(first_row(plane, unit, depth), shells), lanes]

        def send(ref, send_sem, recv_sem, fluid, solid):
            return pltpu.make_async_remote_copy(
                src_ref=ref, dst_ref=ref, send_sem=send_sem, recv_sem=recv_sem,
                device_id=(fluid, solid), device_id_type=MESH,
            )

        def along(d, incoming=False):
            depth = turn(z, -d, nz) if incoming else z
            return send(block(xy, core, depth), s1.at[d - 1], r1.at[d - 1], f, turn(z, d, nz))

        def across(d, e, incoming=False):
            plane = turn(xy, -e, nxy) if incoming else xy
            return send(
                block(plane, core, turn(z, -d, nz)), s2.at[d, e - 1], r2.at[d, e - 1],
                fluid_of(turn(xy, e, nxy), core), z,
            )

        def pair(d, e, incoming=False):
            unit = other if incoming else core
            return send(
                block(turn(xy, -e, nxy), unit, turn(z, -d, nz)), s3.at[d, e], r3.at[d, e],
                fluid_of(xy, other), z,
            )

        for d in range(1, nz):
            along(d).start()
        for d in range(nz):
            if d > 0:
                along(d, True).wait_recv()
            for e in range(1, nxy):
                across(d, e).start()
            pair(d, 0).start()
        for d in range(nz):
            for e in range(1, nxy):
                across(d, e, True).wait_recv()
                pair(d, e).start()
        for d in range(nz):
            for e in range(nxy):
                pair(d, e, True).wait_recv()
        for d in range(1, nz):
            along(d).wait_send()
        for d in range(nz):
            for e in range(1, nxy):
                across(d, e).wait_send()
            for e in range(nxy):
                pair(d, e).wait_send()

    lane = lax.broadcasted_iota(jnp.int32, (1, LANES), 1)

    def pick(vector, q):
        return jnp.sum(jnp.where(lane == q, vector, 0.0), axis=1, keepdims=True)

    def coefficients(j):
        k = j - 1
        total = jnp.sum(slots[j, :, breadth:], axis=0, keepdims=True)
        sc[j] = total
        norm = jnp.sqrt(pick(total, 0) / count + EPSILON)

        @pl.when(j > 0)
        def _():
            norm_out[jnp.maximum(k, 0)] = jnp.broadcast_to(norm, (1, LANES))

        order = ITERS - 1
        gram = [[None] * order for _ in range(order)]
        for col in range(order):
            vector = sc[col + 2]
            for row in range(col + 1):
                value = pick(vector, 8 + row)
                if row == col:
                    value = jnp.where(col < k, value, 1.0)
                gram[col][row] = value
        side = [-pick(total, 1 + i) for i in range(order)]
        lower = [[None] * order for _ in range(order)]
        for row in range(order):
            for col in range(row + 1):
                value = gram[row][col]
                for inner in range(col):
                    value = value - lower[row][inner] * lower[col][inner]
                if row == col:
                    lower[row][row] = jnp.sqrt(value)
                else:
                    lower[row][col] = value / lower[col][col]
        middle = []
        for row in range(order):
            value = side[row]
            for inner in range(row):
                value = value - lower[row][inner] * middle[inner]
            middle.append(value / lower[row][row])
        result = [None] * order
        for row in reversed(range(order)):
            value = middle[row]
            for inner in range(row + 1, order):
                value = value - lower[inner][row] * result[inner]
            result[row] = value / lower[row][row]
        relax = jnp.where(j == 1, jnp.full((1, 1), RELAX - 1.0, f32), 0.0)
        return [relax] + result

    def combine(j, coefs, at):
        value = slots[j, at, 0:breadth]
        before = slots[0, at, 0:breadth]
        for i in range(ITERS):
            after = slots[i + 1, at, 0:breadth]
            value = value + coefs[i] * (after - before)
            before = after
        return value

    def dot(a, b, dims=((1,), (0,))):
        return lax.dot_general(a, b, (dims, ((), ())), preferred_element_type=f32)

    def iteration(j, carry):
        all_gather(j, pl.ds(0, breadth + LANES))
        coefs = coefficients(j)

        def update(i, c):
            at = pl.ds(pl.multiple_of(i * 16, 16), 16)
            curb[at, :] = combine(j, coefs, at).astype(bf16)
            return c

        lax.fori_loop(0, every // 16, update, 0, unroll=2)
        cur_own[...] = combine(j, coefs, pl.ds(own_row, shells))
        picked = None
        for c in range(3):
            term = dot(
                place[:, c * every:(c + 1) * every], curb[:, c * nodes:(c + 1) * nodes]
            )
            picked = term if picked is None else picked + term
        disp[...] = picked

        def fluid(i, c):
            @pl.when(j == 0)
            def _():
                rbf_copy(i).wait()

            loads = []
            for u in range(CHUNK):
                b = i * CHUNK + u
                at = pl.ds(pl.multiple_of(b * 8, 8), 8)
                moved = dot(disp[at, :].astype(bf16), rbf[b], ((1,), (1,)))
                load = (tr_ref[at, :] - ms_ref[at, :] * moved).astype(bf16)
                loadf[at, :] = load.astype(f32)
                loads.append(load)
            for u in range(CHUNK):
                b = i * CHUNK + u
                at = pl.ds(pl.multiple_of(b * 8, 8), 8)
                mapped[at, :] = dot(loads[u], rbf[b]).astype(bf16).astype(f32)
            return c

        lax.fori_loop(0, nchunk, fluid, 0)

        mapped_half = mapped[...].astype(bf16)
        for c in range(3):
            send_a[:, c * nodes:(c + 1) * nodes] = dot(collect[1, c], mapped_half).astype(bf16)
        copy_a = pltpu.make_async_remote_copy(
            src_ref=send_a, dst_ref=recv_a, send_sem=sa, recv_sem=ra,
            device_id=(fluid_of(xy, other), z), device_id_type=MESH,
        )
        copy_a.start()
        for c in range(3):
            part[:, c * nodes:(c + 1) * nodes] = dot(collect[0, c], mapped_half)
        copy_a.wait_recv()
        part[...] = part[...] + recv_a[...].astype(f32)

        def copy_b(e):
            return pltpu.make_async_remote_copy(
                src_ref=send_b.at[e - 1], dst_ref=recv_b.at[e - 1],
                send_sem=sb.at[e - 1], recv_sem=rb.at[e - 1],
                device_id=(fluid_of(turn(xy, e, nxy), core), z), device_id_type=MESH,
            )

        for e in range(1, nxy):
            at = pl.ds(pl.multiple_of(turn(xy, e, nxy) * group, group), group)
            send_b[e - 1] = part[at, :].astype(bf16)
            copy_b(e).start()
        line = part[pl.ds(pl.multiple_of(xy * group, group), group), :]
        for e in range(1, nxy):
            copy_b(e).wait_recv()
            line = line + recv_b[e - 1].astype(f32)
        shell_sum[...] = line

        def copy_c(d):
            return pltpu.make_async_remote_copy(
                src_ref=send_c.at[d - 1], dst_ref=recv_c.at[d - 1],
                send_sem=sc_s.at[d - 1], recv_sem=sc_r.at[d - 1],
                device_id=(f, turn(z, d, nz)), device_id_type=MESH,
            )

        for d in range(1, nz):
            at = pl.ds(pl.multiple_of(turn(z, d, nz) * shells, shells), shells)
            send_c[d - 1] = shell_sum[at, :].astype(bf16)
            copy_c(d).start()
        shell_load = shell_sum[pl.ds(pl.multiple_of(z * shells, shells), shells), :]
        for d in range(1, nz):
            copy_c(d).wait_recv()
            shell_load = shell_load + recv_c[d - 1].astype(f32)
        copy_a.wait_send()
        for e in range(1, nxy):
            copy_b(e).wait_send()
        for d in range(1, nz):
            copy_c(d).wait_send()

        @pl.when(j == 0)
        def _():
            inv_copy().wait()

        current = cur_own[...]
        forcing = (shell_load + robin_ref[...] * current).astype(bf16)
        shell_row = lax.broadcasted_iota(jnp.int32, (shells, breadth), 0)

        def solid(s, image):
            return jnp.where(shell_row == s, dot(forcing, inv[s]), image)

        image = lax.fori_loop(0, shells, solid, jnp.zeros((shells, breadth), f32), unroll=2)
        residual = image - current
        newest = residual - rprev[...]
        rprev[...] = residual
        vhist[lax.rem(j + ITERS - 1, ITERS)] = newest
        lane_rows = lax.broadcasted_iota(jnp.int32, (shells, LANES), 1)

        def put(vector, q, product):
            return jnp.where(lane_rows == q, jnp.sum(product, axis=1, keepdims=True), vector)

        scalars = put(jnp.zeros((shells, LANES), f32), 0, residual * residual)
        for i in range(ITERS - 1):
            scalars = put(scalars, 1 + i, vhist[i] * residual)
            scalars = put(scalars, 8 + i, vhist[i] * newest)
        own = pl.ds(own_row, shells)
        slots[j + 1, own, 0:breadth] = image
        slots[j + 1, own, breadth:] = scalars
        return carry

    lax.fori_loop(0, ITERS, iteration, 0)
    all_gather(ITERS, pl.ds(breadth, LANES))
    cur_out[...] = combine(ITERS, coefficients(ITERS), pl.ds(own_row, shells))
    load_out[...] = loadf[0:blocks * 8, :].astype(bf16)


def fused(nf, nz, rbf_blocks, fluid_traction, fluid_mass, route, slot, shell_inverse, robin_coef, shell_start):
    f32, bf16 = jnp.float32, jnp.bfloat16
    blocks, nodes, _ = rbf_blocks.shape
    shells, breadth = shell_start.shape
    nxy = nf // 2
    group = nz * shells
    every = nf * group
    rows = -(-blocks * 8 // LANES) * LANES
    target = route[:, 0] * shells + slot
    part_of = jnp.arange(8, dtype=jnp.int32)[None, :]
    key = jnp.where(part_of < 3, target[:, None] + part_of * every, -1).reshape(-1)
    key = jnp.pad(key, (0, rows - blocks * 8), constant_values=-1)

    def spread(x):
        return jnp.pad(
            x.reshape(blocks, 3, nodes).astype(f32), ((0, 0), (0, 5), (0, 0))
        ).reshape(blocks * 8, nodes)

    dma = pltpu.SemaphoreType.DMA
    vmem = pl.BlockSpec(memory_space=pltpu.VMEM)
    anywhere = pl.BlockSpec(memory_space=pl.ANY)
    current, load, norms = pl.pallas_call(
        functools.partial(kernel, nf, nz, blocks, nodes, shells, every * breadth),
        out_shape=(
            jax.ShapeDtypeStruct((shells, breadth), f32),
            jax.ShapeDtypeStruct((blocks * 8, nodes), bf16),
            jax.ShapeDtypeStruct((ITERS, 1, LANES), f32),
        ),
        in_specs=[vmem] * 6 + [anywhere] * 2,
        out_specs=(vmem, vmem, vmem),
        scratch_shapes=[
            pltpu.VMEM(rbf_blocks.shape, bf16),
            pltpu.VMEM(shell_inverse.shape, bf16),
            pltpu.VMEM((ITERS + 1, every, breadth + LANES), f32),
            pltpu.VMEM((every, breadth), bf16),
            pltpu.VMEM((shells, breadth), f32),
            pltpu.VMEM((ITERS, shells, breadth), f32),
            pltpu.VMEM((shells, breadth), f32),
            pltpu.VMEM((ITERS + 1, 1, LANES), f32),
            pltpu.VMEM((rows, 3 * every), bf16),
            pltpu.VMEM((2, 3, nxy * group, rows), bf16),
            pltpu.VMEM((rows, nodes), f32),
            pltpu.VMEM((rows, nodes), f32),
            pltpu.VMEM((rows, nodes), f32),
            pltpu.VMEM((nxy * group, breadth), f32),
            pltpu.VMEM((nxy * group, breadth), bf16),
            pltpu.VMEM((nxy * group, breadth), bf16),
            pltpu.VMEM((nxy - 1, group, breadth), bf16),
            pltpu.VMEM((nxy - 1, group, breadth), bf16),
            pltpu.VMEM((nz - 1, shells, breadth), bf16),
            pltpu.VMEM((nz - 1, shells, breadth), bf16),
            pltpu.VMEM((group, breadth), f32),
            dma((blocks // CHUNK,)),
            dma,
            dma((nz - 1,)), dma((nz - 1,)),
            dma((nz, nxy - 1)), dma((nz, nxy - 1)),
            dma((nz, nxy)), dma((nz, nxy)),
            dma, dma,
            dma((nxy - 1,)), dma((nxy - 1,)),
            dma((nz - 1,)), dma((nz - 1,)),
        ],
        compiler_params=pltpu.CompilerParams(
            collective_id=0, has_side_effects=True, vmem_limit_bytes=VMEM_BYTES
        ),
        name="coupling",
    )(
        key[:, None], key[None, :], spread(fluid_traction), spread(fluid_mass),
        robin_coef, shell_start, rbf_blocks, shell_inverse,
    )
    load = load.reshape(blocks, 8, nodes)[:, :3].reshape(blocks, breadth)
    return current, load, norms[:, 0, 0]


def choose(nf, nz):
    def body(rbf_blocks, *others):
        if nf * nz > 32:
            return per_device(rbf_blocks, *others)
        return fused(nf, nz, rbf_blocks, *others)

    return body


def solution(mesh):
    in_specs = (
        P(("fluid", "solid"), None, None),
        P(("fluid", "solid"), None),
        P(("fluid", "solid"), None),
        P(("fluid", "solid"), None),
        P(("fluid", "solid")),
        P(("fluid", "solid"), None, None),
        P(("fluid", "solid"), None),
        P(("fluid", "solid"), None),
    )
    out_specs = (P(("fluid", "solid"), None), P(("fluid", "solid"), None), P())
    return jax.shard_map(
        choose(mesh.shape["fluid"], mesh.shape["solid"]), mesh=mesh, in_specs=in_specs, out_specs=out_specs, check_vma=False
    )
```

profile of v0, /device:TPU:0, one launch (start us, length us, event | category | flops | bytes accessed | tf_op | source)
XLA Modules:
  0.0 198.8 jit_solution(4164234690780727081)
XLA Ops:
  0.6 0.7 bitcast_add_fusion
  1.3 0.1 add_select_fusion
  1.4 0.1 select_n.9
  1.5 0.6 broadcast_in_dim.23.row_ref
  2.1 1.1 copy.18
  3.2 0.2 copy.19
  3.4 1.1 copy.20
  4.4 0.2 copy.21
  4.6 0.9 broadcast_in_dim.24.key_ref
  5.6 1.3 bitcast_convert_fusion
  6.9 187.1 %coupling.1 = (f32[8,768]{1,0:T(8,128)}, bf16[832,256]{1,0:T(8,128)(2,1)}, f32[6,1,128]{2,1,0:T(1,128)}) custom-call(s32[896,1]{1,0:T(8,128)} %broadcast_in_dim.24.key_ref, s32[1,896]{1,0:T(1,128)} %broadcast_in_dim.23.row_ref, f32[832,256]{1,0:T(8,128)} %get-tuple-element.16.tr_ref, f32[832,256]{1,0:T(8,128)} %get-tuple-element.15.ms_ref, ...), custom_call_target="tpu_custom_call" | custom-call | tf_op jit(solution)/shard_map/coupling/pallas_call | solution.py:499
  194.1 1.1 slice.8
  195.1 0.2 copy.25
  195.3 0.8 copy.24
  196.2 1.3 slice_reduce_fusion
  197.5 1.3 copy.27
  (3 shorter events, 0.0 us)
where the time goes:
time: 199 us
  Pallas kernels  187 us (94%)
  local copies, waits for them, and re-layouts  8.87 us (4%)
  other arithmetic  2.1 us (1%)
    pallas_call x1, Pallas kernels, fused(): pl.pallas_call(functools.partial(kernel, nf, nz, blocks, nodes, shells, e...  187 us
    unnamed x5, local copies, waits for them, and re-layouts  4.51 us

commit v1 on v0

v1 whole, which is shorter than its diff:
```python
import functools

import jax
import jax.numpy as jnp
from jax import lax
from jax.experimental import pallas as pl
from jax.experimental.pallas import tpu as pltpu
from jax.sharding import PartitionSpec as P

ITERS = 6


RELAX = 0.3
EPSILON = 1e-06


def transport(buffer, devices, capacity):
    breadth = buffer.shape[1]
    moved = lax.all_to_all(
        buffer.reshape(devices, capacity, breadth),
        ("fluid", "solid"),
        split_axis=0,
        concat_axis=0,
        tiled=True,
    )
    return moved.reshape(devices * capacity, breadth)


def least_squares(gram, target_side):
    order = gram.shape[0]
    lower = [[None] * order for _ in range(order)]
    for row in range(order):
        for column in range(row + 1):
            total = gram[row, column]
            for inner in range(column):
                total = total - lower[row][inner] * lower[column][inner]
            if row == column:
                lower[row][row] = jnp.sqrt(total)
            else:
                lower[row][column] = total / lower[column][column]
    middle = []
    for row in range(order):
        total = target_side[row]
        for inner in range(row):
            total = total - lower[row][inner] * middle[inner]
        middle.append(total / lower[row][row])
    result = [None] * order
    for row in reversed(range(order)):
        total = middle[row]
        for inner in range(row + 1, order):
            total = total - lower[inner][row] * result[inner]
        result[row] = total / lower[row][row]
    return jnp.stack(result)


def per_device(
    rbf_blocks, fluid_traction, fluid_mass, route, slot, shell_inverse, robin_coef, shell_start
):
    devices = lax.axis_size("fluid") * lax.axis_size("solid")
    blocks = rbf_blocks.shape[0]
    nodes = rbf_blocks.shape[1]
    breadth = 3 * nodes
    shells = shell_inverse.shape[0]
    capacity = max(2, 2 * blocks // devices)
    slots_all = devices * capacity
    destination = route[:, 0]
    block_order = jnp.arange(blocks, dtype=jnp.int32)
    earlier = (destination[:, None] == destination[None, :]) & (
        block_order[None, :] < block_order[:, None]
    )
    slot_rank = jnp.sum(earlier.astype(jnp.int32), axis=1)
    position = destination * capacity + slot_rank
    positions = jnp.arange(slots_all, dtype=jnp.int32)
    placing = positions[:, None] == position[None, :]
    place_out = placing.astype(jnp.bfloat16)
    place_in = (position[:, None] == positions[None, :]).astype(jnp.bfloat16)
    wanted = jnp.max(jnp.where(placing, slot[None, :] + 1, 0), axis=1) - 1
    asked = lax.all_to_all(
        wanted.reshape(devices, capacity),
        ("fluid", "solid"),
        split_axis=0,
        concat_axis=0,
        tiled=True,
    ).reshape(slots_all)
    shell_ids = jnp.arange(shells, dtype=jnp.int32)
    picking = (asked[:, None] == shell_ids[None, :]).astype(jnp.bfloat16)
    collecting = (shell_ids[:, None] == asked[None, :]).astype(jnp.bfloat16)
    traction = fluid_traction.astype(jnp.float32)
    massive = fluid_mass.astype(jnp.float32)
    count = shells * devices * breadth
    current = shell_start
    residuals = []
    images = []
    norms = []
    last_load = None
    for iteration in range(ITERS):
        current_half = current.astype(jnp.bfloat16)
        outgoing = jnp.dot(picking, current_half, preferred_element_type=jnp.float32).astype(
            jnp.bfloat16
        )
        incoming = transport(outgoing, devices, capacity)
        displaced = jnp.dot(place_in, incoming, preferred_element_type=jnp.float32).astype(
            jnp.bfloat16
        )
        moved = jnp.einsum(
            "bcj,bij->bci",
            displaced.reshape(blocks, 3, nodes),
            rbf_blocks,
            preferred_element_type=jnp.float32,
        ).reshape(blocks, breadth)
        load = (traction - massive * moved).astype(jnp.bfloat16)
        last_load = load
        mapped = (
            jnp.einsum(
                "bci,bij->bcj",
                load.reshape(blocks, 3, nodes),
                rbf_blocks,
                preferred_element_type=jnp.float32,
            )
            .reshape(blocks, breadth)
            .astype(jnp.bfloat16)
        )
        sending = jnp.dot(place_out, mapped, preferred_element_type=jnp.float32).astype(
            jnp.bfloat16
        )
        arrived = transport(sending, devices, capacity)
        shell_load = jnp.dot(collecting, arrived, preferred_element_type=jnp.float32)
        forcing = (shell_load + robin_coef * current).astype(jnp.bfloat16)
        image = jnp.einsum("bi,bij->bj", forcing, shell_inverse, preferred_element_type=jnp.float32)
        residual = image - current
        residuals.append(residual)
        images.append(image)
        squares_local = jnp.sum(residual * residual)
        if iteration == 0:
            gram_local = jnp.zeros((1, 1), jnp.float32)
            rhs_local = jnp.zeros((1,), jnp.float32)
        else:
            changes = jnp.stack(
                [(residuals[i + 1] - residuals[i]).reshape(-1) for i in range(iteration)]
            )
            gram_local = jnp.dot(changes, changes.T, precision=lax.Precision.HIGHEST)
            rhs_local = jnp.dot(changes, residual.reshape(-1), precision=lax.Precision.HIGHEST)
        gram, rhs, squares = lax.psum((gram_local, rhs_local, squares_local), ("fluid", "solid"))
        norms.append(jnp.sqrt(squares / count + EPSILON))
        if iteration == 0:
            current = current + RELAX * residual
        else:
            image_changes = jnp.stack([images[i + 1] - images[i] for i in range(iteration)])
            coefs = least_squares(gram, -rhs)
            current = image + jnp.tensordot(
                coefs, image_changes, axes=1, precision=lax.Precision.HIGHEST
            )
    return (current, last_load, jnp.stack(norms))


CHUNK = 52
LANES = 128
VMEM_BYTES = 67043328
MESH = pl.DeviceIdType.MESH


def kernel(
    nf, nz, blocks, nodes, shells, count,
    tgt_ref, tr_ref, ms_ref, robin_ref, start_ref, rbf_hbm, inv_hbm,
    cur_out, load_out, norm_out,
    rbf, inv, gath, scal, xcur, xprev, pprev, cur, rprev, wx, wp, vhist, sc, cb,
    place, collect, tr8, ms8, disp8, map8, moved, mapn, part,
    send_a, recv_a, send_b, recv_b,
    rbf_sem, inv_sem, ag_s, ag_r, pr_s, pr_r, sl_s, sl_r, ra_s, ra_r, rb_s, rb_r,
):
    f32, bf16 = jnp.float32, jnp.bfloat16
    breadth = 3 * nodes
    nxy = nf // 2
    nx = 2 if nxy % 2 == 0 else 1
    ny = nxy // nx
    chips = nxy * nz
    half = chips * shells
    group = nz * shells
    f = lax.axis_index("fluid")
    z = lax.axis_index("solid")
    core = lax.rem(f, 2)
    other = 1 - core
    xy = f // 2
    x, y = lax.rem(xy, nx), xy // nx
    nchunk = blocks // CHUNK
    ngroup = blocks // 8
    parts = nodes // LANES

    def hops(step):
        ey, ex, ez = step
        return min(ey, ny - ey) + min(ex, nx - ex) + min(ez, nz - ez)

    steps = sorted(
        [(ey, ex, ez) for ey in range(ny) for ex in range(nx) for ez in range(nz) if ey + ex + ez],
        key=hops, reverse=True,
    )
    far = len(steps)

    def away(step, sign=1):
        ey, ex, ez = step
        plane = lax.rem(y + sign * ey + ny, ny) * nx + lax.rem(x + sign * ex + nx, nx)
        return plane, lax.rem(z + sign * ez + nz, nz)

    targets = [away(s) for s in steps]
    sources = [away(s, -1) for s in steps]

    def chip(plane, depth):
        return plane * nz + depth

    me = chip(xy, z)

    def remote(src, dst, send_sem, recv_sem, plane, unit, depth):
        return pltpu.make_async_remote_copy(
            src_ref=src, dst_ref=dst, send_sem=send_sem, recv_sem=recv_sem,
            device_id=(plane * 2 + unit, depth), device_id_type=MESH,
        )

    def rbf_copy(i):
        at = pl.ds(i * CHUNK, CHUNK)
        return pltpu.make_async_copy(rbf_hbm.at[at], rbf.at[at], rbf_sem.at[i])

    def inv_copy():
        return pltpu.make_async_copy(inv_hbm, inv, inv_sem)

    for i in range(nchunk):
        rbf_copy(i).start()
    inv_copy().start()

    barrier = pltpu.get_barrier_semaphore()
    for plane, depth in targets + [(xy, z)]:
        for unit in (core, other):
            if plane is xy and unit is core:
                continue
            pl.semaphore_signal(
                barrier, inc=1, device_id=(plane * 2 + unit, depth), device_id_type=MESH
            )

    xcur[...] = start_ref[...]
    for ref in (xprev, pprev, cur, rprev, wx, wp, vhist, sc, cb):
        ref[...] = jnp.zeros(ref.shape, ref.dtype)
    mapn[...] = jnp.zeros(mapn.shape, bf16)

    def clear(i, c):
        at = pl.ds(pl.multiple_of(i * 64, 64), 64)
        for ref in (tr8, ms8, disp8):
            ref[:, at, :] = jnp.zeros((parts, 64, LANES), f32)
        return c

    lax.fori_loop(0, ngroup, clear, 0)

    def strided(q, c):
        return pl.ds(q * 64 + c, 8, stride=8)

    def scatter(ref, q, c, value):
        for p in range(parts):
            ref[p, strided(q, c), :] = value[:, p * LANES:(p + 1) * LANES]

    def gather(ref, q, c):
        return jnp.concatenate([ref[p, strided(q, c), :] for p in range(parts)], axis=1)

    def rows_of(ref, at):
        return jnp.concatenate([ref[p, at, :] for p in range(parts)], axis=1)

    def set_rows(ref, at, value):
        for p in range(parts):
            ref[p, at, :] = value[:, p * LANES:(p + 1) * LANES]

    for src, dst in ((tr_ref, tr8), (ms_ref, ms8)):
        for row in range(0, blocks, 16):
            size = min(16, blocks - row)
            wide = src[row:row + size, :].astype(f32)
            for k in range(size // 8):
                for c in range(3):
                    scatter(dst, row // 8 + k, c, wide[k * 8:(k + 1) * 8, c * nodes:(c + 1) * nodes])

    target = tgt_ref[...]
    diagonal = lax.broadcasted_iota(jnp.int32, (blocks, blocks), 0) == lax.broadcasted_iota(
        jnp.int32, (blocks, blocks), 1
    )
    column = jnp.sum(jnp.where(diagonal, target.astype(f32), 0.0), axis=1, keepdims=True)
    for side in range(2):
        unit = core if side == 0 else other
        line = lax.broadcasted_iota(jnp.int32, (half, 1), 0)
        ids = (line // group * 2 + unit) * group + lax.rem(line, group)
        collect[side] = jnp.zeros(collect.shape[1:], bf16)
        collect[side, :, 0:blocks] = jnp.where(ids == target, 1.0, 0.0).astype(bf16)
        lane = lax.broadcasted_iota(jnp.int32, (1, half), 1)
        ids = (lane // group * 2 + unit) * group + lax.rem(lane, group)
        place[side] = jnp.where(ids.astype(f32) == column, 1.0, 0.0).astype(bf16)

    pl.semaphore_wait(barrier, 2 * far + 1)

    lane = lax.broadcasted_iota(jnp.int32, (1, LANES), 1)

    def pick(vector, q):
        return jnp.sum(jnp.where(lane == q, vector, 0.0), axis=1, keepdims=True)

    def dot(a, b, dims=((1,), (0,))):
        return lax.dot_general(a, b, (dims, ((), ())), preferred_element_type=f32)

    def ag(j, k, incoming=False):
        at = chip(*sources[k]) if incoming else me
        block = gath.at[j, core, at]
        return remote(block, block, ag_s.at[k], ag_r.at[k], targets[k][0], core, targets[k][1])

    def ag_pair(j, k, incoming=False):
        at = me if k == far else chip(*sources[k])
        block = gath.at[j, other if incoming else core, at]
        return remote(block, block, pr_s.at[k], pr_r.at[k], xy, other, z)

    def scalar_copies(j, incoming=False):
        copies = []
        turn = lax.rem(j, 2)
        for k in range(far + 1):
            for unit in range(2):
                if k == far and unit == 0:
                    continue
                at = (me if k == far else chip(*sources[k])) if incoming else me
                mine = (core if unit == 0 else other) if incoming else core
                plane, depth = (xy, z) if k == far else targets[k]
                block = scal.at[j, mine, at]
                copies.append(remote(
                    block, block, sl_s.at[turn, k, unit], sl_r.at[turn, k, unit],
                    plane, core if unit == 0 else other, depth,
                ))
        return copies

    def scalars(j):
        residual = xcur[...] - cur[...]
        newest = residual - rprev[...]
        rprev[...] = residual
        vhist[lax.rem(j + ITERS + ITERS - 2, ITERS)] = jnp.where(j > 0, newest, 0.0)

        def total(product):
            return jnp.sum(jnp.sum(product, axis=0, keepdims=True), axis=1, keepdims=True)

        vector = jnp.where(lane == 0, total(residual * residual), 0.0)
        for i in range(ITERS - 1):
            vector = jnp.where(lane == 1 + i, total(vhist[i] * residual), vector)
            vector = jnp.where(lane == 8 + i, total(vhist[i] * newest), vector)
        scal[j, core, me] = jnp.where(j > 0, vector, 0.0)
        for copy in scalar_copies(j):
            copy.start()

    def coefficients(j):
        for copy in scalar_copies(j, True):
            copy.wait_recv()
        k = j - 1
        total = jnp.sum(jnp.sum(scal[j], axis=0), axis=0)
        sc[j] = total
        norm = jnp.sqrt(pick(total, 0) / count + EPSILON)

        @pl.when(j > 0)
        def _():
            norm_out[jnp.maximum(k, 0)] = jnp.broadcast_to(norm, (1, LANES))

        order = ITERS - 1
        gram = [[None] * order for _ in range(order)]
        for col in range(order):
            vector = sc[col + 2]
            for row in range(col + 1):
                value = pick(vector, 8 + row)
                if row == col:
                    value = jnp.where(col < k, value, 1.0)
                gram[col][row] = value
        side = [-pick(total, 1 + i) for i in range(order)]
        lower = [[None] * order for _ in range(order)]
        for row in range(order):
            for col in range(row + 1):
                value = gram[row][col]
                for inner in range(col):
                    value = value - lower[row][inner] * lower[col][inner]
                if row == col:
                    lower[row][row] = jnp.sqrt(value)
                else:
                    lower[row][col] = value / lower[col][col]
        middle = []
        for row in range(order):
            value = side[row]
            for inner in range(row):
                value = value - lower[row][inner] * middle[inner]
            middle.append(value / lower[row][row])
        result = [None] * order
        for row in reversed(range(order)):
            value = middle[row]
            for inner in range(row + 1, order):
                value = value - lower[inner][row] * result[inner]
            result[row] = value / lower[row][row]
        relax = jnp.where(j == 1, jnp.full((1, 1), RELAX - 1.0, f32), 0.0)
        for i, value in enumerate([relax] + result):
            cb[i] = jnp.broadcast_to(value, (1, LANES))

    def weight(i):
        return jnp.concatenate([cb[i]] * (breadth // LANES), axis=1)

    def blend(newest, history):
        value = newest
        for i in range(ITERS):
            value = value + weight(i) * history[i]
        return value

    def note(j):
        wx[lax.rem(j + ITERS - 1, ITERS)] = xcur[...] - xprev[...]
        xprev[...] = xcur[...]

    def iteration(j, carry):
        gath[j, core, me] = xcur[...].astype(bf16)
        for k in range(far):
            ag(j, k).start()
        ag_pair(j, far).start()
        scalars(j)
        note(j)
        for k in reversed(range(far)):
            ag(j, k, True).wait_recv()
            ag_pair(j, k).start()

        def image_half(unit):
            return gath[j, unit].astype(f32).reshape(half, breadth).astype(bf16)

        picked = dot(place[0], image_half(core))
        for k in range(far + 1):
            ag_pair(j, k, True).wait_recv()
        picked = picked + dot(place[1], image_half(other))
        for q in range(ngroup):
            for c in range(3):
                scatter(disp8, q, c, picked[q * 8:(q + 1) * 8, c * nodes:(c + 1) * nodes])

        def fluid(i, c):
            @pl.when(j == 0)
            def _():
                rbf_copy(i).wait()

            loads = []
            for u in range(CHUNK):
                b = i * CHUNK + u
                at = pl.ds(pl.multiple_of(b * 8, 8), 8)
                shift = dot(rows_of(disp8, at).astype(bf16), rbf[b], ((1,), (1,)))
                set_rows(moved.at[j], at, shift)
                loads.append((rows_of(tr8, at) - rows_of(ms8, at) * shift).astype(bf16))
            for u in range(CHUNK):
                b = i * CHUNK + u
                at = pl.ds(pl.multiple_of(b * 8, 8), 8)
                set_rows(map8, at, dot(loads[u], rbf[b]))
            return c

        lax.fori_loop(0, nchunk, fluid, 0)

        for q in range(0, ngroup, 2):
            size = min(2, ngroup - q)
            for c in range(3):
                rows = [gather(map8, q + k, c) for k in range(size)]
                value = jnp.concatenate(rows, axis=0) if size > 1 else rows[0]
                mapn[q * 8:(q + size) * 8, c * nodes:(c + 1) * nodes] = value.astype(bf16)
        send_a[...] = dot(collect[1], mapn[...]).reshape(chips, shells, breadth).astype(bf16)
        copy_a = remote(send_a, recv_a, ra_s, ra_r, xy, other, z)
        copy_a.start()
        part[...] = dot(collect[0], mapn[...]).reshape(chips, shells, breadth)
        copy_a.wait_recv()

        def copy_b(k):
            return remote(
                send_b.at[k], recv_b.at[k], rb_s.at[k], rb_r.at[k], targets[k][0], core, targets[k][1]
            )

        for k in range(far):
            at = chip(*targets[k])
            send_b[k] = (part[at] + recv_a[at].astype(f32)).astype(bf16)
            copy_b(k).start()
        shell_load = part[me] + recv_a[me].astype(f32)

        coefficients(j)
        cur[...] = blend(xcur[...], wx)
        for k in range(far):
            ag(j, k).wait_send()
        for k in range(far + 1):
            ag_pair(j, k).wait_send()
        for copy in scalar_copies(j):
            copy.wait_send()
        copy_a.wait_send()

        @pl.when(j == 0)
        def _():
            inv_copy().wait()

        for k in reversed(range(far)):
            copy_b(k).wait_recv()
            shell_load = shell_load + recv_b[k].astype(f32)
        forcing = (shell_load + robin_ref[...] * xcur[...]).astype(bf16)
        shell_row = lax.broadcasted_iota(jnp.int32, (shells, breadth), 0)
        image = jnp.zeros((shells, breadth), f32)
        for s in range(shells):
            image = jnp.where(shell_row == s, dot(forcing, inv[s]), image)
        wp[lax.rem(j + ITERS - 1, ITERS)] = image - pprev[...]
        pprev[...] = image
        xcur[...] = blend(image, wp)
        for k in range(far):
            copy_b(k).wait_send()
        return carry

    lax.fori_loop(0, ITERS, iteration, 0)
    scalars(ITERS)
    note(ITERS)
    weights = []
    for i in range(ITERS):
        value = 1.0 if i == ITERS - 1 else -cb[i]
        value = value + cb[i - 1] if i > 0 else value
        weights.append(jnp.concatenate([value] * (nodes // LANES), axis=1))
    for q in range(0, ngroup, 2):
        size = min(2, ngroup - q)
        rows = slice(q * 8, (q + size) * 8)
        for c in range(3):
            shift = None
            for i in range(ITERS):
                term = [gather(moved.at[i], q + k, c) for k in range(size)]
                term = weights[i] * (jnp.concatenate(term, axis=0) if size > 1 else term[0])
                shift = term if shift is None else shift + term
            lanes = slice(c * nodes, (c + 1) * nodes)
            load = tr_ref[rows, lanes].astype(f32) - ms_ref[rows, lanes].astype(f32) * shift
            load_out[rows, lanes] = load.astype(bf16)
    coefficients(ITERS)
    cur_out[...] = blend(xcur[...], wx)
    for copy in scalar_copies(ITERS):
        copy.wait_send()


def fused(nf, nz, rbf_blocks, fluid_traction, fluid_mass, route, slot, shell_inverse, robin_coef, shell_start):
    f32, bf16 = jnp.float32, jnp.bfloat16
    blocks, nodes, _ = rbf_blocks.shape
    shells, breadth = shell_start.shape
    chips = nf // 2 * nz
    half = chips * shells
    far = chips - 1
    target = (route[:, 0] * shells + slot)[None, :]
    padded = -(-blocks // LANES) * LANES
    dma = pltpu.SemaphoreType.DMA
    vmem = pl.BlockSpec(memory_space=pltpu.VMEM)
    anywhere = pl.BlockSpec(memory_space=pl.ANY)
    state = pltpu.VMEM((shells, breadth), f32)
    history = pltpu.VMEM((ITERS, shells, breadth), f32)
    wide = pltpu.VMEM((nodes // LANES, blocks * 8, LANES), f32)
    current, load, norms = pl.pallas_call(
        functools.partial(kernel, nf, nz, blocks, nodes, shells, 2 * half * breadth),
        out_shape=(
            jax.ShapeDtypeStruct((shells, breadth), f32),
            jax.ShapeDtypeStruct((blocks, breadth), bf16),
            jax.ShapeDtypeStruct((ITERS, 1, LANES), f32),
        ),
        in_specs=[vmem] * 5 + [anywhere] * 2,
        out_specs=(vmem, vmem, vmem),
        scratch_shapes=[
            pltpu.VMEM(rbf_blocks.shape, bf16),
            pltpu.VMEM(shell_inverse.shape, bf16),
            pltpu.VMEM((ITERS, 2, chips, shells, breadth), bf16),
            pltpu.VMEM((ITERS + 1, 2, chips, 1, LANES), f32),
            state, state, state, state, state,
            history, history, history,
            pltpu.VMEM((ITERS + 1, 1, LANES), f32),
            pltpu.VMEM((ITERS, 1, LANES), f32),
            pltpu.VMEM((2, blocks, half), bf16),
            pltpu.VMEM((2, half, padded), bf16),
            wide, wide, wide, wide,
            pltpu.VMEM((ITERS, nodes // LANES, blocks * 8, LANES), f32),
            pltpu.VMEM((padded, breadth), bf16),
            pltpu.VMEM((chips, shells, breadth), f32),
            pltpu.VMEM((chips, shells, breadth), bf16),
            pltpu.VMEM((chips, shells, breadth), bf16),
            pltpu.VMEM((far, shells, breadth), bf16),
            pltpu.VMEM((far, shells, breadth), bf16),
            dma((blocks // CHUNK,)),
            dma,
            dma((far,)), dma((far,)),
            dma((far + 1,)), dma((far + 1,)),
            dma((2, far + 1, 2)), dma((2, far + 1, 2)),
            dma, dma,
            dma((far,)), dma((far,)),
        ],
        compiler_params=pltpu.CompilerParams(
            collective_id=0, has_side_effects=True, vmem_limit_bytes=VMEM_BYTES
        ),
        name="coupling",
    )(
        target, fluid_traction, fluid_mass, robin_coef, shell_start, rbf_blocks, shell_inverse,
    )
    return current, load, norms[:, 0, 0]


def choose(nf, nz):
    def body(rbf_blocks, *others):
        if nf * nz > 32:
            return per_device(rbf_blocks, *others)
        return fused(nf, nz, rbf_blocks, *others)

    return body


def solution(mesh):
    in_specs = (
        P(("fluid", "solid"), None, None),
        P(("fluid", "solid"), None),
        P(("fluid", "solid"), None),
        P(("fluid", "solid"), None),
        P(("fluid", "solid")),
        P(("fluid", "solid"), None, None),
        P(("fluid", "solid"), None),
        P(("fluid", "solid"), None),
    )
    out_specs = (P(("fluid", "solid"), None), P(("fluid", "solid"), None), P())
    return jax.shard_map(
        choose(mesh.shape["fluid"], mesh.shape["solid"]), mesh=mesh, in_specs=in_specs, out_specs=out_specs, check_vma=False
    )
```

time: 199 us -> 152 us (0.76)
  Pallas kernels: 187 us -> 146 us
  local copies, waits for them, and re-layouts: 8.87 us -> 4.24 us
    pallas_call x1, Pallas kernels: 187 us -> 146 us  [fused(): pl.pallas_call(functools.partial(kernel, nf, nz, blocks, nodes, shells, 2...]
    unnamed x5 -> x2, local copies, waits for them, and re-layouts: 4.51 us -> 2.93 us
where the time goes in v1:
time: 152 us
  Pallas kernels  146 us (96%)
  local copies, waits for them, and re-layouts  4.24 us (3%)
    pallas_call x1, Pallas kernels, fused(): pl.pallas_call(functools.partial(kernel, nf, nz, blocks, nodes, shells, 2...  146 us

profile of v1, /device:TPU:0, one launch (start us, length us, event | category | flops | bytes accessed | tf_op | source)
XLA Modules:
  0.0 151.8 jit_solution(14152513855172907706)
XLA Ops:
  0.6 1.2 fusion.tgt_ref
  1.8 145.7 %coupling.1 = (f32[8,768]{1,0:T(8,128)}, bf16[104,768]{1,0:T(8,128)(2,1)}, f32[6,1,128]{2,1,0:T(1,128)}) custom-call(s32[1,104]{1,0:T(1,128)} %fusion.tgt_ref, bf16[104,768]{1,0:T(8,128)(2,1)} %tr_ref.1, bf16[104,768]{1,0:T(8,128)(2,1)} %ms_ref.1, f32[8,768]{1,0:T(8,128)} %robin_ref.1, f32[8,768]{1,0:T(8,128)} %start_ref.1, bf16[104,256,256]{2,1,0:T(8,128)(2,1)} %rbf_hbm.1, ...), custom_call_target="tpu_custom_call" | custom-call | tf_op jit(solution)/shard_map/coupling/pallas_call | solution.py:541
  147.5 1.3 slice_reduce_fusion
  148.8 1.3 copy.13
  150.2 1.6 %copy.14 = bf16[104,768]{1,0:T(8,128)(2,1)} copy(bf16[104,768]{1,0:T(8,128)(2,1)} %get-tuple-element.13) | data formatting | bytes 319488

commit v2 on v1

--- a/solution.py
+++ b/solution.py
@@ -154,6 +154,8 @@
 
 
 CHUNK = 52
+LOAD = 13
+TURN = 4
 LANES = 128
 VMEM_BYTES = 67043328
 MESH = pl.DeviceIdType.MESH
@@ -161,12 +163,13 @@
 
 def kernel(
     nf, nz, blocks, nodes, shells, count,
-    tgt_ref, tr_ref, ms_ref, robin_ref, start_ref, rbf_hbm, inv_hbm,
+    start_ref, route_hbm, slot_hbm, tr_hbm, ms_hbm, robin_hbm, rbf_hbm, inv_hbm,
     cur_out, load_out, norm_out,
-    rbf, inv, gath, scal, xcur, xprev, pprev, cur, rprev, wx, wp, vhist, sc, cb,
-    place, collect, tr8, ms8, disp8, map8, moved, mapn, part,
+    route_ref, slot_ref, tr_ref, ms_ref, robin_ref, load_buf,
+    rbf, flip, inv, gath, scal, xcur, xprev, pprev, cur, rprev, wx, wp, vhist, sc, cb,
+    place, collect, tr8, ms8, disp8, map8, load8, moved, mapn, part,
     send_a, recv_a, send_b, recv_b,
-    rbf_sem, inv_sem, ag_s, ag_r, pr_s, pr_r, sl_s, sl_r, ra_s, ra_r, rb_s, rb_r,
+    in_sem, out_sem, rbf_sem, inv_sem, ag_s, ag_r, pr_s, pr_r, sl_s, sl_r, ra_s, ra_r, rb_s, rb_r,
 ):
     f32, bf16 = jnp.float32, jnp.bfloat16
     breadth = 3 * nodes
@@ -183,6 +186,7 @@
     xy = f // 2
     x, y = lax.rem(xy, nx), xy // nx
     nchunk = blocks // CHUNK
+    nload = blocks // LOAD
     ngroup = blocks // 8
     parts = nodes // LANES
 
@@ -216,13 +220,22 @@
         )
 
     def rbf_copy(i):
-        at = pl.ds(i * CHUNK, CHUNK)
+        at = pl.ds(i * LOAD, LOAD)
         return pltpu.make_async_copy(rbf_hbm.at[at], rbf.at[at], rbf_sem.at[i])
 
     def inv_copy():
         return pltpu.make_async_copy(inv_hbm, inv, inv_sem)
 
-    for i in range(nchunk):
+    smalls = [
+        pltpu.make_async_copy(src, dst, in_sem.at[i])
+        for i, (src, dst) in enumerate((
+            (route_hbm, route_ref), (slot_hbm, slot_ref), (tr_hbm, tr_ref), (ms_hbm, ms_ref),
+            (robin_hbm, robin_ref),
+        ))
+    ]
+    for copy in smalls:
+        copy.start()
+    for i in range(nload):
         rbf_copy(i).start()
     inv_copy().start()
 
@@ -235,8 +248,28 @@
                 barrier, inc=1, device_id=(plane * 2 + unit, depth), device_id_type=MESH
             )
 
+    def ag(j, k, incoming=False):
+        at = chip(*sources[k]) if incoming else me
+        block = gath.at[j, core, at]
+        return remote(block, block, ag_s.at[k], ag_r.at[k], targets[k][0], core, targets[k][1])
+
+    def ag_pair(j, k, incoming=False):
+        at = me if k == far else chip(*sources[k])
+        block = gath.at[j, other if incoming else core, at]
+        return remote(block, block, pr_s.at[k], pr_r.at[k], xy, other, z)
+
+    def share(j):
+        gath[j, core, me] = xcur[...].astype(bf16)
+        for k in range(far):
+            ag(j, k).start()
+        ag_pair(j, far).start()
+
     xcur[...] = start_ref[...]
-    for ref in (xprev, pprev, cur, rprev, wx, wp, vhist, sc, cb):
+    pl.semaphore_wait(barrier, 2 * far + 1)
+    share(0)
+
+    xprev[...] = start_ref[...]
+    for ref in (pprev, cur, rprev, wx, wp, vhist, sc, cb):
         ref[...] = jnp.zeros(ref.shape, ref.dtype)
     mapn[...] = jnp.zeros(mapn.shape, bf16)
 
@@ -247,6 +280,8 @@
         return c
 
     lax.fori_loop(0, ngroup, clear, 0)
+    for copy in smalls:
+        copy.wait()
 
     def strided(q, c):
         return pl.ds(q * 64 + c, 8, stride=8)
@@ -273,23 +308,21 @@
                 for c in range(3):
                     scatter(dst, row // 8 + k, c, wide[k * 8:(k + 1) * 8, c * nodes:(c + 1) * nodes])
 
-    target = tgt_ref[...]
     diagonal = lax.broadcasted_iota(jnp.int32, (blocks, blocks), 0) == lax.broadcasted_iota(
         jnp.int32, (blocks, blocks), 1
     )
-    column = jnp.sum(jnp.where(diagonal, target.astype(f32), 0.0), axis=1, keepdims=True)
+    target = (route_ref[...] * shells + slot_ref[...]).astype(f32)
+    column = jnp.sum(jnp.where(diagonal, target, 0.0), axis=1, keepdims=True)
     for side in range(2):
         unit = core if side == 0 else other
         line = lax.broadcasted_iota(jnp.int32, (half, 1), 0)
         ids = (line // group * 2 + unit) * group + lax.rem(line, group)
         collect[side] = jnp.zeros(collect.shape[1:], bf16)
-        collect[side, :, 0:blocks] = jnp.where(ids == target, 1.0, 0.0).astype(bf16)
+        collect[side, :, 0:blocks] = jnp.where(ids.astype(f32) == target, 1.0, 0.0).astype(bf16)
         lane = lax.broadcasted_iota(jnp.int32, (1, half), 1)
         ids = (lane // group * 2 + unit) * group + lax.rem(lane, group)
         place[side] = jnp.where(ids.astype(f32) == column, 1.0, 0.0).astype(bf16)
 
-    pl.semaphore_wait(barrier, 2 * far + 1)
-
     lane = lax.broadcasted_iota(jnp.int32, (1, LANES), 1)
 
     def pick(vector, q):
@@ -297,16 +330,6 @@
 
     def dot(a, b, dims=((1,), (0,))):
         return lax.dot_general(a, b, (dims, ((), ())), preferred_element_type=f32)
-
-    def ag(j, k, incoming=False):
-        at = chip(*sources[k]) if incoming else me
-        block = gath.at[j, core, at]
-        return remote(block, block, ag_s.at[k], ag_r.at[k], targets[k][0], core, targets[k][1])
-
-    def ag_pair(j, k, incoming=False):
-        at = me if k == far else chip(*sources[k])
-        block = gath.at[j, other if incoming else core, at]
-        return remote(block, block, pr_s.at[k], pr_r.at[k], xy, other, z)
 
     def scalar_copies(j, incoming=False):
         copies = []
@@ -329,7 +352,7 @@
         residual = xcur[...] - cur[...]
         newest = residual - rprev[...]
         rprev[...] = residual
-        vhist[lax.rem(j + ITERS + ITERS - 2, ITERS)] = jnp.where(j > 0, newest, 0.0)
+        vhist[lax.rem(j + ITERS - 2, ITERS)] = newest
 
         def total(product):
             return jnp.sum(jnp.sum(product, axis=0, keepdims=True), axis=1, keepdims=True)
@@ -338,7 +361,7 @@
         for i in range(ITERS - 1):
             vector = jnp.where(lane == 1 + i, total(vhist[i] * residual), vector)
             vector = jnp.where(lane == 8 + i, total(vhist[i] * newest), vector)
-        scal[j, core, me] = jnp.where(j > 0, vector, 0.0)
+        scal[j, core, me] = vector
         for copy in scalar_copies(j):
             copy.start()
 
@@ -350,9 +373,7 @@
         sc[j] = total
         norm = jnp.sqrt(pick(total, 0) / count + EPSILON)
 
-        @pl.when(j > 0)
-        def _():
-            norm_out[jnp.maximum(k, 0)] = jnp.broadcast_to(norm, (1, LANES))
+        norm_out[k] = jnp.broadcast_to(norm, (1, LANES))
 
         order = ITERS - 1
         gram = [[None] * order for _ in range(order)]
@@ -404,12 +425,6 @@
         xprev[...] = xcur[...]
 
     def iteration(j, carry):
-        gath[j, core, me] = xcur[...].astype(bf16)
-        for k in range(far):
-            ag(j, k).start()
-        ag_pair(j, far).start()
-        scalars(j)
-        note(j)
         for k in reversed(range(far)):
             ag(j, k, True).wait_recv()
             ag_pair(j, k).start()
@@ -425,25 +440,38 @@
             for c in range(3):
                 scatter(disp8, q, c, picked[q * 8:(q + 1) * 8, c * nodes:(c + 1) * nodes])
 
-        def fluid(i, c):
-            @pl.when(j == 0)
-            def _():
+        def move(i, size, table, dims):
+            for u in range(size):
+                b = i * size + u
+                at = pl.ds(pl.multiple_of(b * 8, 8), 8)
+                shift = dot(rows_of(disp8, at).astype(bf16), table[b], dims)
+                set_rows(moved.at[j], at, shift)
+                load8[b] = (rows_of(tr8, at) - rows_of(ms8, at) * shift).astype(bf16)
+
+        @pl.when(j == 0)
+        def _():
+            def first(i, c):
                 rbf_copy(i).wait()
-
-            loads = []
+                move(i, LOAD, rbf, ((1,), (1,)))
+                return c
+
+            lax.fori_loop(0, nload, first, 0)
+
+        @pl.when(j > 0)
+        def _():
+            def later(i, c):
+                move(i, CHUNK, flip, ((1,), (0,)))
+                return c
+
+            lax.fori_loop(0, nchunk, later, 0)
+
+        def back(i, c):
             for u in range(CHUNK):
                 b = i * CHUNK + u
-                at = pl.ds(pl.multiple_of(b * 8, 8), 8)
-                shift = dot(rows_of(disp8, at).astype(bf16), rbf[b], ((1,), (1,)))
-                set_rows(moved.at[j], at, shift)
-                loads.append((rows_of(tr8, at) - rows_of(ms8, at) * shift).astype(bf16))
-            for u in range(CHUNK):
-                b = i * CHUNK + u
-                at = pl.ds(pl.multiple_of(b * 8, 8), 8)
-                set_rows(map8, at, dot(loads[u], rbf[b]))
+                set_rows(map8, pl.ds(pl.multiple_of(b * 8, 8), 8), dot(load8[b], rbf[b]))
             return c
 
-        lax.fori_loop(0, nchunk, fluid, 0)
+        lax.fori_loop(0, nchunk, back, 0)
 
         for q in range(0, ngroup, 2):
             size = min(2, ngroup - q)
@@ -468,18 +496,27 @@
             copy_b(k).start()
         shell_load = part[me] + recv_a[me].astype(f32)
 
-        coefficients(j)
+        @pl.when(j > 0)
+        def _():
+            coefficients(j)
+            for copy in scalar_copies(j):
+                copy.wait_send()
+
         cur[...] = blend(xcur[...], wx)
         for k in range(far):
             ag(j, k).wait_send()
         for k in range(far + 1):
             ag_pair(j, k).wait_send()
-        for copy in scalar_copies(j):
-            copy.wait_send()
         copy_a.wait_send()
 
         @pl.when(j == 0)
         def _():
+            def turn(i, c):
+                for u in range(TURN):
+                    flip[i * TURN + u] = rbf[i * TURN + u].T
+                return c
+
+            lax.fori_loop(0, blocks // TURN, turn, 0)
             inv_copy().wait()
 
         for k in reversed(range(far)):
@@ -493,13 +530,18 @@
         wp[lax.rem(j + ITERS - 1, ITERS)] = image - pprev[...]
         pprev[...] = image
         xcur[...] = blend(image, wp)
+
+        @pl.when(j < ITERS - 1)
+        def _():
+            share(j + 1)
+
+        scalars(j + 1)
+        note(j + 1)
         for k in range(far):
             copy_b(k).wait_send()
         return carry
 
     lax.fori_loop(0, ITERS, iteration, 0)
-    scalars(ITERS)
-    note(ITERS)
     weights = []
     for i in range(ITERS):
         value = 1.0 if i == ITERS - 1 else -cb[i]
@@ -516,11 +558,21 @@
                 shift = term if shift is None else shift + term
             lanes = slice(c * nodes, (c + 1) * nodes)
             load = tr_ref[rows, lanes].astype(f32) - ms_ref[rows, lanes].astype(f32) * shift
-            load_out[rows, lanes] = load.astype(bf16)
+            load_buf[rows, lanes] = load.astype(bf16)
+    write = pltpu.make_async_copy(load_buf, load_out, out_sem)
+    write.start()
     coefficients(ITERS)
     cur_out[...] = blend(xcur[...], wx)
     for copy in scalar_copies(ITERS):
         copy.wait_send()
+    write.wait()
+
+
+def hand_over(current, load, norms, current_out, load_out, norm_out):
+    current_out[...] = current[...]
+    load_out[...] = load[...]
+    for i in range(norm_out.shape[0]):
+        norm_out[i] = norms[i, 0, 0]
 
 
 def fused(nf, nz, rbf_blocks, fluid_traction, fluid_mass, route, slot, shell_inverse, robin_coef, shell_start):
@@ -530,7 +582,6 @@
     chips = nf // 2 * nz
     half = chips * shells
     far = chips - 1
-    target = (route[:, 0] * shells + slot)[None, :]
     padded = -(-blocks // LANES) * LANES
     dma = pltpu.SemaphoreType.DMA
     vmem = pl.BlockSpec(memory_space=pltpu.VMEM)
@@ -545,9 +596,16 @@
             jax.ShapeDtypeStruct((blocks, breadth), bf16),
             jax.ShapeDtypeStruct((ITERS, 1, LANES), f32),
         ),
-        in_specs=[vmem] * 5 + [anywhere] * 2,
-        out_specs=(vmem, vmem, vmem),
+        in_specs=[vmem] + [anywhere] * 7,
+        out_specs=(vmem, anywhere, vmem),
         scratch_shapes=[
+            pltpu.VMEM((1, blocks), jnp.int32),
+            pltpu.VMEM((1, blocks), jnp.int32),
+            pltpu.VMEM((blocks, breadth), bf16),
+            pltpu.VMEM((blocks, breadth), bf16),
+            state,
+            pltpu.VMEM((blocks, breadth), bf16),
+            pltpu.VMEM(rbf_blocks.shape, bf16),
             pltpu.VMEM(rbf_blocks.shape, bf16),
             pltpu.VMEM(shell_inverse.shape, bf16),
             pltpu.VMEM((ITERS, 2, chips, shells, breadth), bf16),
@@ -559,6 +617,7 @@
             pltpu.VMEM((2, blocks, half), bf16),
             pltpu.VMEM((2, half, padded), bf16),
             wide, wide, wide, wide,
+            pltpu.VMEM((blocks, 8, nodes), bf16),
             pltpu.VMEM((ITERS, nodes // LANES, blocks * 8, LANES), f32),
             pltpu.VMEM((padded, breadth), bf16),
             pltpu.VMEM((chips, shells, breadth), f32),
@@ -566,7 +625,8 @@
             pltpu.VMEM((chips, shells, breadth), bf16),
             pltpu.VMEM((far, shells, breadth), bf16),
             pltpu.VMEM((far, shells, breadth), bf16),
-            dma((blocks // CHUNK,)),
+            dma((5,)), dma,
+            dma((blocks // LOAD,)),
             dma,
             dma((far,)), dma((far,)),
             dma((far + 1,)), dma((far + 1,)),
@@ -579,9 +639,21 @@
         ),
         name="coupling",
     )(
-        target, fluid_traction, fluid_mass, robin_coef, shell_start, rbf_blocks, shell_inverse,
+        shell_start, route.T, slot[None, :], fluid_traction, fluid_mass, robin_coef, rbf_blocks,
+        shell_inverse,
     )
-    return current, load, norms[:, 0, 0]
+    smem = pl.BlockSpec(memory_space=pltpu.SMEM)
+    return pl.pallas_call(
+        hand_over,
+        out_shape=(
+            jax.ShapeDtypeStruct(current.shape, f32),
+            jax.ShapeDtypeStruct(load.shape, bf16),
+            jax.ShapeDtypeStruct((ITERS,), f32),
+        ),
+        in_specs=[vmem, vmem, smem],
+        out_specs=(vmem, vmem, smem),
+        name="results",
+    )(current, load, norms)
 
 
 def choose(nf, nz):

time: 152 us -> 140 us (0.921)
  Pallas kernels: 146 us -> 139 us
  local copies, waits for them, and re-layouts: 4.24 us -> 0 us
    pallas_call x1, Pallas kernels: 146 us -> 137 us  [fused(): pl.pallas_call(functools.partial(kernel, nf, nz, blocks, nodes, shells, 2...]
    unnamed x2 -> x0, local copies, waits for them, and re-layouts: 2.93 us -> none
    pallas_call x0 -> x1, Pallas kernels: none -> 1.63 us  [fused(): pl.pallas_call(hand_over, out_shape=(jax.ShapeDtypeStruct(current.shape,...]
where the time goes in v2:
time: 140 us
  Pallas kernels  139 us (99%)
    pallas_call x1, Pallas kernels, fused(): pl.pallas_call(functools.partial(kernel, nf, nz, blocks, nodes, shells, 2...  137 us

profile of v2, /device:TPU:0, one launch (start us, length us, event | category | flops | bytes accessed | tf_op | source)
XLA Modules:
  0.0 139.5 jit_solution(1905187391613843630)
XLA Ops:
  0.6 137.3 %coupling.1 = (f32[8,768]{1,0:T(8,128)}, bf16[104,768]{1,0:T(8,128)(2,1)}, f32[6,1,128]{2,1,0:T(1,128)}) custom-call(f32[8,768]{1,0:T(8,128)} %start_ref.1, s32[1,104]{1,0:T(1,128)} %bitcast.2, s32[1,104]{1,0:T(1,128)} %bitcast.3, bf16[104,768]{1,0:T(8,128)(2,1)} %tr_hbm.1, bf16[104,768]{1,0:T(8,128)(2,1)} %ms_hbm.1, f32[8,768]{1,0:T(8,128)} %robin_hbm.1, ...), custom_call_target="tpu_custom_call" | custom-call | tf_op jit(solution)/shard_map/coupling/pallas_call | solution.py:592
  137.9 1.6 %results.1 = (f32[8,768]{1,0:T(8,128)}, bf16[104,768]{1,0:T(8,128)(2,1)}, f32[6]{0:T(128)}) custom-call(f32[8,768]{1,0:T(8,128)} %get-tuple-element.6.current, bf16[104,768]{1,0:T(8,128)(2,1)} %get-tuple-element.7.load, f32[6,1,128]{2,1,0:T(1,128)} %get-tuple-element.8.norms), custom_call_target="tpu_custom_call" | custom-call | tf_op jit(solution)/shard_map/results/pallas_call | solution.py:646

commit v3 on v2

--- a/solution.py
+++ b/solution.py
@@ -154,7 +154,8 @@
 
 
 CHUNK = 52
-LOAD = 13
+LOAD = 26
+TAIL = 52
 TURN = 4
 LANES = 128
 VMEM_BYTES = 67043328
@@ -163,15 +164,17 @@
 
 def kernel(
     nf, nz, blocks, nodes, shells, count,
-    start_ref, route_hbm, slot_hbm, tr_hbm, ms_hbm, robin_hbm, rbf_hbm, inv_hbm,
+    start_hbm, route_hbm, slot_hbm, tr_hbm, ms_hbm, robin_hbm, rbf_hbm, inv_hbm,
     cur_out, load_out, norm_out,
-    route_ref, slot_ref, tr_ref, ms_ref, robin_ref, load_buf,
-    rbf, flip, inv, gath, scal, xcur, xprev, pprev, cur, rprev, wx, wp, vhist, sc, cb,
+    start_ref, route_ref, slot_ref, tr_ref, ms_ref, robin_ref, load_buf,
+    rbf, flip, inv, gath, scal, xcur, xprev, pprev, cur, rprev, robin, wx, wp, vhist, sc, cb,
     place, collect, tr8, ms8, disp8, map8, load8, moved, mapn, part,
     send_a, recv_a, send_b, recv_b,
     in_sem, out_sem, rbf_sem, inv_sem, ag_s, ag_r, pr_s, pr_r, sl_s, sl_r, ra_s, ra_r, rb_s, rb_r,
 ):
     f32, bf16 = jnp.float32, jnp.bfloat16
+    parts = nodes // LANES
+    thin = 3 * LANES
     breadth = 3 * nodes
     nxy = nf // 2
     nx = 2 if nxy % 2 == 0 else 1
@@ -188,7 +191,6 @@
     nchunk = blocks // CHUNK
     nload = blocks // LOAD
     ngroup = blocks // 8
-    parts = nodes // LANES
 
     def hops(step):
         ey, ex, ez = step
@@ -218,26 +220,6 @@
             src_ref=src, dst_ref=dst, send_sem=send_sem, recv_sem=recv_sem,
             device_id=(plane * 2 + unit, depth), device_id_type=MESH,
         )
-
-    def rbf_copy(i):
-        at = pl.ds(i * LOAD, LOAD)
-        return pltpu.make_async_copy(rbf_hbm.at[at], rbf.at[at], rbf_sem.at[i])
-
-    def inv_copy():
-        return pltpu.make_async_copy(inv_hbm, inv, inv_sem)
-
-    smalls = [
-        pltpu.make_async_copy(src, dst, in_sem.at[i])
-        for i, (src, dst) in enumerate((
-            (route_hbm, route_ref), (slot_hbm, slot_ref), (tr_hbm, tr_ref), (ms_hbm, ms_ref),
-            (robin_hbm, robin_ref),
-        ))
-    ]
-    for copy in smalls:
-        copy.start()
-    for i in range(nload):
-        rbf_copy(i).start()
-    inv_copy().start()
 
     barrier = pltpu.get_barrier_semaphore()
     for plane, depth in targets + [(xy, z)]:
@@ -248,27 +230,66 @@
                 barrier, inc=1, device_id=(plane * 2 + unit, depth), device_id_type=MESH
             )
 
-    def ag(j, k, incoming=False):
+    def rbf_copy(i):
+        at = pl.ds(i * LOAD, LOAD)
+        return pltpu.make_async_copy(rbf_hbm.at[at], rbf.at[at], rbf_sem.at[i])
+
+    def inv_copy():
+        return pltpu.make_async_copy(inv_hbm, inv, inv_sem)
+
+    smalls = [
+        pltpu.make_async_copy(src, dst, in_sem.at[i])
+        for i, (src, dst) in enumerate((
+            (start_hbm, start_ref), (route_hbm, route_ref), (slot_hbm, slot_ref), (tr_hbm, tr_ref),
+            (ms_hbm, ms_ref), (robin_hbm, robin_ref),
+        ))
+    ]
+    for copy in smalls:
+        copy.start()
+    for i in range(nload):
+        rbf_copy(i).start()
+    inv_copy().start()
+
+    def lanes_of(c, h):
+        return slice(c * nodes + h * LANES, c * nodes + (h + 1) * LANES)
+
+    def thin_of(c):
+        return slice(c * LANES, (c + 1) * LANES)
+
+    def halved(ref, h):
+        return jnp.concatenate([ref[:, lanes_of(c, h)] for c in range(3)], axis=1)
+
+    def ag(j, h, k, incoming=False):
         at = chip(*sources[k]) if incoming else me
-        block = gath.at[j, core, at]
-        return remote(block, block, ag_s.at[k], ag_r.at[k], targets[k][0], core, targets[k][1])
-
-    def ag_pair(j, k, incoming=False):
+        block = gath.at[j, h, core, at]
+        return remote(
+            block, block, ag_s.at[h, k], ag_r.at[h, k], targets[k][0], core, targets[k][1]
+        )
+
+    def ag_pair(j, h, k, incoming=False):
         at = me if k == far else chip(*sources[k])
-        block = gath.at[j, other if incoming else core, at]
-        return remote(block, block, pr_s.at[k], pr_r.at[k], xy, other, z)
-
-    def share(j):
-        gath[j, core, me] = xcur[...].astype(bf16)
+        block = gath.at[j, h, other if incoming else core, at]
+        return remote(block, block, pr_s.at[h, k], pr_r.at[h, k], xy, other, z)
+
+    def share(j, h):
+        gath[j, h, core, me] = xcur[h].astype(bf16)
         for k in range(far):
-            ag(j, k).start()
-        ag_pair(j, far).start()
-
-    xcur[...] = start_ref[...]
+            ag(j, h, k).start()
+        ag_pair(j, h, far).start()
+
+    def relay(j, h):
+        for k in reversed(range(far)):
+            ag(j, h, k, True).wait_recv()
+            ag_pair(j, h, k).start()
+
+    smalls[0].wait()
+    for h in range(parts):
+        xcur[h] = halved(start_ref, h)
     pl.semaphore_wait(barrier, 2 * far + 1)
-    share(0)
-
-    xprev[...] = start_ref[...]
+    for h in range(parts):
+        share(0, h)
+
+    xprev[...] = xcur[...]
     for ref in (pprev, cur, rprev, wx, wp, vhist, sc, cb):
         ref[...] = jnp.zeros(ref.shape, ref.dtype)
     mapn[...] = jnp.zeros(mapn.shape, bf16)
@@ -280,18 +301,13 @@
         return c
 
     lax.fori_loop(0, ngroup, clear, 0)
-    for copy in smalls:
+    for copy in smalls[1:]:
         copy.wait()
+    for h in range(parts):
+        robin[h] = halved(robin_ref, h)
 
     def strided(q, c):
         return pl.ds(q * 64 + c, 8, stride=8)
-
-    def scatter(ref, q, c, value):
-        for p in range(parts):
-            ref[p, strided(q, c), :] = value[:, p * LANES:(p + 1) * LANES]
-
-    def gather(ref, q, c):
-        return jnp.concatenate([ref[p, strided(q, c), :] for p in range(parts)], axis=1)
 
     def rows_of(ref, at):
         return jnp.concatenate([ref[p, at, :] for p in range(parts)], axis=1)
@@ -306,7 +322,8 @@
             wide = src[row:row + size, :].astype(f32)
             for k in range(size // 8):
                 for c in range(3):
-                    scatter(dst, row // 8 + k, c, wide[k * 8:(k + 1) * 8, c * nodes:(c + 1) * nodes])
+                    for h in range(parts):
+                        dst[h, strided(row // 8 + k, c), :] = wide[k * 8:(k + 1) * 8, lanes_of(c, h)]
 
     diagonal = lax.broadcasted_iota(jnp.int32, (blocks, blocks), 0) == lax.broadcasted_iota(
         jnp.int32, (blocks, blocks), 1
@@ -355,7 +372,8 @@
         vhist[lax.rem(j + ITERS - 2, ITERS)] = newest
 
         def total(product):
-            return jnp.sum(jnp.sum(product, axis=0, keepdims=True), axis=1, keepdims=True)
+            rows = jnp.sum(jnp.sum(product, axis=0), axis=0, keepdims=True)
+            return jnp.sum(rows, axis=1, keepdims=True)
 
         vector = jnp.where(lane == 0, total(residual * residual), 0.0)
         for i in range(ITERS - 1):
@@ -372,7 +390,6 @@
         total = jnp.sum(jnp.sum(scal[j], axis=0), axis=0)
         sc[j] = total
         norm = jnp.sqrt(pick(total, 0) / count + EPSILON)
-
         norm_out[k] = jnp.broadcast_to(norm, (1, LANES))
 
         order = ITERS - 1
@@ -411,90 +428,138 @@
         for i, value in enumerate([relax] + result):
             cb[i] = jnp.broadcast_to(value, (1, LANES))
 
-    def weight(i):
-        return jnp.concatenate([cb[i]] * (breadth // LANES), axis=1)
-
-    def blend(newest, history):
+    def blend(newest, history, h):
         value = newest
         for i in range(ITERS):
-            value = value + weight(i) * history[i]
+            value = value + jnp.concatenate([cb[i]] * 3, axis=1) * history[i, h]
         return value
 
     def note(j):
         wx[lax.rem(j + ITERS - 1, ITERS)] = xcur[...] - xprev[...]
         xprev[...] = xcur[...]
 
+    upper = lax.broadcasted_iota(jnp.int32, (16, LANES), 0) < 8
+
     def iteration(j, carry):
-        for k in reversed(range(far)):
-            ag(j, k, True).wait_recv()
-            ag_pair(j, k).start()
-
-        def image_half(unit):
-            return gath[j, unit].astype(f32).reshape(half, breadth).astype(bf16)
-
-        picked = dot(place[0], image_half(core))
-        for k in range(far + 1):
-            ag_pair(j, k, True).wait_recv()
-        picked = picked + dot(place[1], image_half(other))
-        for q in range(ngroup):
-            for c in range(3):
-                scatter(disp8, q, c, picked[q * 8:(q + 1) * 8, c * nodes:(c + 1) * nodes])
-
-        def move(i, size, table, dims):
-            for u in range(size):
+        def fetch(h):
+            def side(unit):
+                return gath[j, h, unit].astype(f32).reshape(half, thin).astype(bf16)
+
+            picked = dot(place[0], side(core))
+            for k in range(far + 1):
+                ag_pair(j, h, k, True).wait_recv()
+            picked = picked + dot(place[1], side(other))
+            for q in range(ngroup):
+                for c in range(3):
+                    disp8[h, strided(q, c), :] = picked[q * 8:(q + 1) * 8, thin_of(c)]
+
+        def move(i, size, h, turned):
+            cut = slice(h * LANES, (h + 1) * LANES)
+            for u in range(0, size, 2):
                 b = i * size + u
-                at = pl.ds(pl.multiple_of(b * 8, 8), 8)
-                shift = dot(rows_of(disp8, at).astype(bf16), table[b], dims)
+                at = pl.ds(pl.multiple_of(b * 8, 16), 16)
+                both = disp8[h, at, :]
+                left = jnp.concatenate(
+                    [jnp.where(upper, both, 0.0), jnp.where(upper, 0.0, both)], axis=1
+                ).astype(bf16)
+                if turned:
+                    shift = dot(left, jnp.concatenate([flip[b, cut, :], flip[b + 1, cut, :]], axis=0))
+                else:
+                    right = jnp.concatenate([rbf[b, :, cut], rbf[b + 1, :, cut]], axis=1)
+                    shift = dot(left, right, ((1,), (1,)))
+                if h > 0:
+                    shift = shift + rows_of(moved.at[j], at)
                 set_rows(moved.at[j], at, shift)
-                load8[b] = (rows_of(tr8, at) - rows_of(ms8, at) * shift).astype(bf16)
-
-        @pl.when(j == 0)
-        def _():
-            def first(i, c):
-                rbf_copy(i).wait()
-                move(i, LOAD, rbf, ((1,), (1,)))
+                if h == parts - 1:
+                    load = rows_of(tr8, at) - rows_of(ms8, at) * shift
+                    load8[i * (size // 2) + u // 2] = load.astype(bf16)
+
+        def forward(h):
+            @pl.when(j == 0)
+            def _():
+                def first(i, c):
+                    if h == 0:
+                        rbf_copy(i).wait()
+
+                        @pl.when(i == nload // 2)
+                        def _():
+                            relay(j, 1)
+
+                    move(i, LOAD, h, False)
+                    return c
+
+                lax.fori_loop(0, nload, first, 0)
+
+            @pl.when(j > 0)
+            def _():
+                def later(i, c):
+                    if h == 0:
+                        @pl.when(i == nchunk // 2)
+                        def _():
+                            relay(j, 1)
+
+                    move(i, CHUNK, h, True)
+                    return c
+
+                lax.fori_loop(0, nchunk, later, 0)
+
+        def backward(h, size):
+            cut = slice(h * LANES, (h + 1) * LANES)
+
+            def back(i, c):
+                if h > 0:
+                    @pl.when(i == blocks // size - 1)
+                    def _():
+                        spread_out(h - 1)
+
+                for u in range(0, size, 2):
+                    b = i * size + u
+                    at = pl.multiple_of(b * 8, 16)
+                    right = jnp.concatenate([rbf[b, :, cut], rbf[b + 1, :, cut]], axis=1)
+                    both = dot(load8[i * (size // 2) + u // 2], right)
+                    map8[h, pl.ds(at, 8), :] = both[0:8, 0:LANES]
+                    map8[h, pl.ds(at + 8, 8), :] = both[8:16, LANES:2 * LANES]
                 return c
 
-            lax.fori_loop(0, nload, first, 0)
-
-        @pl.when(j > 0)
-        def _():
-            def later(i, c):
-                move(i, CHUNK, flip, ((1,), (0,)))
-                return c
-
-            lax.fori_loop(0, nchunk, later, 0)
-
-        def back(i, c):
-            for u in range(CHUNK):
-                b = i * CHUNK + u
-                set_rows(map8, pl.ds(pl.multiple_of(b * 8, 8), 8), dot(load8[b], rbf[b]))
-            return c
-
-        lax.fori_loop(0, nchunk, back, 0)
-
-        for q in range(0, ngroup, 2):
-            size = min(2, ngroup - q)
-            for c in range(3):
-                rows = [gather(map8, q + k, c) for k in range(size)]
-                value = jnp.concatenate(rows, axis=0) if size > 1 else rows[0]
-                mapn[q * 8:(q + size) * 8, c * nodes:(c + 1) * nodes] = value.astype(bf16)
-        send_a[...] = dot(collect[1], mapn[...]).reshape(chips, shells, breadth).astype(bf16)
-        copy_a = remote(send_a, recv_a, ra_s, ra_r, xy, other, z)
-        copy_a.start()
-        part[...] = dot(collect[0], mapn[...]).reshape(chips, shells, breadth)
-        copy_a.wait_recv()
-
-        def copy_b(k):
+            lax.fori_loop(0, blocks // size, back, 0)
+
+        def copy_a(h):
+            return remote(send_a.at[h], recv_a.at[h], ra_s.at[h], ra_r.at[h], xy, other, z)
+
+        def copy_b(h, k):
             return remote(
-                send_b.at[k], recv_b.at[k], rb_s.at[k], rb_r.at[k], targets[k][0], core, targets[k][1]
+                send_b.at[h, k], recv_b.at[h, k], rb_s.at[h, k], rb_r.at[h, k],
+                targets[k][0], core, targets[k][1],
             )
 
-        for k in range(far):
-            at = chip(*targets[k])
-            send_b[k] = (part[at] + recv_a[at].astype(f32)).astype(bf16)
-            copy_b(k).start()
-        shell_load = part[me] + recv_a[me].astype(f32)
+        def gather_up(h):
+            for q in range(0, ngroup, 2):
+                size = min(2, ngroup - q)
+                for c in range(3):
+                    rows = [map8[h, strided(q + k, c), :] for k in range(size)]
+                    value = jnp.concatenate(rows, axis=0) if size > 1 else rows[0]
+                    mapn[h, q * 8:(q + size) * 8, thin_of(c)] = value.astype(bf16)
+            send_a[h] = dot(collect[1], mapn[h]).reshape(chips, shells, thin).astype(bf16)
+            copy_a(h).start()
+            part[h] = dot(collect[0], mapn[h]).reshape(chips, shells, thin)
+
+        def spread_out(h):
+            copy_a(h).wait_recv()
+            for k in range(far):
+                at = chip(*targets[k])
+                send_b[h, k] = (part[h, at] + recv_a[h, at].astype(f32)).astype(bf16)
+                copy_b(h, k).start()
+
+        relay(j, 0)
+        fetch(0)
+        forward(0)
+        fetch(1)
+        forward(1)
+        backward(0, CHUNK)
+        gather_up(0)
+        backward(1, TAIL)
+        gather_up(1)
+        spread_out(1)
 
         @pl.when(j > 0)
         def _():
@@ -502,12 +567,14 @@
             for copy in scalar_copies(j):
                 copy.wait_send()
 
-        cur[...] = blend(xcur[...], wx)
-        for k in range(far):
-            ag(j, k).wait_send()
-        for k in range(far + 1):
-            ag_pair(j, k).wait_send()
-        copy_a.wait_send()
+        for h in range(parts):
+            cur[h] = blend(xcur[h], wx, h)
+        for h in range(parts):
+            for k in range(far):
+                ag(j, h, k).wait_send()
+            for k in range(far + 1):
+                ag_pair(j, h, k).wait_send()
+            copy_a(h).wait_send()
 
         @pl.when(j == 0)
         def _():
@@ -519,26 +586,74 @@
             lax.fori_loop(0, blocks // TURN, turn, 0)
             inv_copy().wait()
 
-        for k in reversed(range(far)):
-            copy_b(k).wait_recv()
-            shell_load = shell_load + recv_b[k].astype(f32)
-        forcing = (shell_load + robin_ref[...] * xcur[...]).astype(bf16)
+        def forcing(h):
+            shell_load = part[h, me] + recv_a[h, me].astype(f32)
+            for k in reversed(range(far)):
+                copy_b(h, k).wait_recv()
+                shell_load = shell_load + recv_b[h, k].astype(f32)
+            return (shell_load + robin[h] * xcur[h]).astype(bf16)
+
+        def table(s, c, h, lanes):
+            return inv[s, lanes_of(c, h), lanes]
+
+        row = lax.broadcasted_iota(jnp.int32, (shells, LANES), 0)
+
+        def tail_left(force, s):
+            last = force[:, thin_of(2)].astype(f32)
+            return jnp.concatenate(
+                [jnp.where(row == s, last, 0.0), jnp.where(row == s + 1, last, 0.0)], axis=1
+            )
+
+        def tail_right(s, h, lanes):
+            return jnp.concatenate([table(s, 2, h, lanes), table(s + 1, 2, h, lanes)], axis=0)
+
+        def lead_right(s, h, lanes):
+            return jnp.concatenate([table(s, 0, h, lanes), table(s, 1, h, lanes)], axis=0)
+
+        force = forcing(0)
         shell_row = lax.broadcasted_iota(jnp.int32, (shells, breadth), 0)
-        image = jnp.zeros((shells, breadth), f32)
+        whole = slice(0, breadth)
+        early = jnp.zeros((shells, breadth), f32)
         for s in range(shells):
-            image = jnp.where(shell_row == s, dot(forcing, inv[s]), image)
-        wp[lax.rem(j + ITERS - 1, ITERS)] = image - pprev[...]
-        pprev[...] = image
-        xcur[...] = blend(image, wp)
-
-        @pl.when(j < ITERS - 1)
-        def _():
-            share(j + 1)
+            lead = dot(force[:, 0:2 * LANES], lead_right(s, 0, whole))
+            early = jnp.where(shell_row == s, lead, early)
+        for s in range(0, shells, 2):
+            early = early + dot(tail_left(force, s).astype(bf16), tail_right(s, 0, whole))
+        force = forcing(1)
+        shell_row = lax.broadcasted_iota(jnp.int32, (shells, thin), 0)
+        for h in range(parts):
+            def wide_right(pieces):
+                return jnp.concatenate(
+                    [make(lanes_of(c, h)) for make in pieces for c in range(3)], axis=1
+                )
+
+            image = jnp.zeros((shells, thin), f32)
+            for s in range(0, shells, 2):
+                both = dot(force[:, 0:2 * LANES], wide_right(
+                    [functools.partial(lead_right, s, 1), functools.partial(lead_right, s + 1, 1)]
+                ))
+                image = jnp.where(shell_row == s, both[:, 0:thin], image)
+                image = jnp.where(shell_row == s + 1, both[:, thin:2 * thin], image)
+            for s in range(0, shells, 4):
+                left = jnp.concatenate([tail_left(force, s), tail_left(force, s + 2)], axis=0)
+                both = dot(left.astype(bf16), wide_right(
+                    [functools.partial(tail_right, s, 1), functools.partial(tail_right, s + 2, 1)]
+                ))
+                image = image + both[0:shells, 0:thin] + both[shells:2 * shells, thin:2 * thin]
+            image = image + jnp.concatenate([early[:, lanes_of(c, h)] for c in range(3)], axis=1)
+            wp[lax.rem(j + ITERS - 1, ITERS), h] = image - pprev[h]
+            pprev[h] = image
+            xcur[h] = blend(image, wp, h)
+
+            @pl.when(j < ITERS - 1)
+            def _():
+                share(j + 1, h)
 
         scalars(j + 1)
         note(j + 1)
-        for k in range(far):
-            copy_b(k).wait_send()
+        for h in range(parts):
+            for k in range(far):
+                copy_b(h, k).wait_send()
         return carry
 
     lax.fori_loop(0, ITERS, iteration, 0)
@@ -546,23 +661,27 @@
     for i in range(ITERS):
         value = 1.0 if i == ITERS - 1 else -cb[i]
         value = value + cb[i - 1] if i > 0 else value
-        weights.append(jnp.concatenate([value] * (nodes // LANES), axis=1))
+        weights.append(value)
     for q in range(0, ngroup, 2):
         size = min(2, ngroup - q)
         rows = slice(q * 8, (q + size) * 8)
         for c in range(3):
-            shift = None
-            for i in range(ITERS):
-                term = [gather(moved.at[i], q + k, c) for k in range(size)]
-                term = weights[i] * (jnp.concatenate(term, axis=0) if size > 1 else term[0])
-                shift = term if shift is None else shift + term
-            lanes = slice(c * nodes, (c + 1) * nodes)
-            load = tr_ref[rows, lanes].astype(f32) - ms_ref[rows, lanes].astype(f32) * shift
-            load_buf[rows, lanes] = load.astype(bf16)
+            for h in range(parts):
+                shift = None
+                for i in range(ITERS):
+                    term = [moved[i, h, strided(q + k, c), :] for k in range(size)]
+                    term = weights[i] * (jnp.concatenate(term, axis=0) if size > 1 else term[0])
+                    shift = term if shift is None else shift + term
+                lanes = lanes_of(c, h)
+                load = tr_ref[rows, lanes].astype(f32) - ms_ref[rows, lanes].astype(f32) * shift
+                load_buf[rows, lanes] = load.astype(bf16)
     write = pltpu.make_async_copy(load_buf, load_out, out_sem)
     write.start()
     coefficients(ITERS)
-    cur_out[...] = blend(xcur[...], wx)
+    for h in range(parts):
+        last = blend(xcur[h], wx, h)
+        for c in range(3):
+            cur_out[:, lanes_of(c, h)] = last[:, thin_of(c)]
     for copy in scalar_copies(ITERS):
         copy.wait_send()
     write.wait()
@@ -586,9 +705,13 @@
     dma = pltpu.SemaphoreType.DMA
     vmem = pl.BlockSpec(memory_space=pltpu.VMEM)
     anywhere = pl.BlockSpec(memory_space=pl.ANY)
-    state = pltpu.VMEM((shells, breadth), f32)
-    history = pltpu.VMEM((ITERS, shells, breadth), f32)
-    wide = pltpu.VMEM((nodes // LANES, blocks * 8, LANES), f32)
+    parts = nodes // LANES
+    thin = 3 * LANES
+    plain = pltpu.VMEM((shells, breadth), f32)
+    state = pltpu.VMEM((parts, shells, thin), f32)
+    history = pltpu.VMEM((ITERS, parts, shells, thin), f32)
+    wide = pltpu.VMEM((parts, blocks * 8, LANES), f32)
+    exchange = pltpu.VMEM((parts, chips, shells, thin), bf16)
     current, load, norms = pl.pallas_call(
         functools.partial(kernel, nf, nz, blocks, nodes, shells, 2 * half * breadth),
         out_shape=(
@@ -596,43 +719,41 @@
             jax.ShapeDtypeStruct((blocks, breadth), bf16),
             jax.ShapeDtypeStruct((ITERS, 1, LANES), f32),
         ),
-        in_specs=[vmem] + [anywhere] * 7,
+        in_specs=[anywhere] * 8,
         out_specs=(vmem, anywhere, vmem),
         scratch_shapes=[
+            plain,
             pltpu.VMEM((1, blocks), jnp.int32),
             pltpu.VMEM((1, blocks), jnp.int32),
             pltpu.VMEM((blocks, breadth), bf16),
             pltpu.VMEM((blocks, breadth), bf16),
-            state,
+            plain,
             pltpu.VMEM((blocks, breadth), bf16),
             pltpu.VMEM(rbf_blocks.shape, bf16),
             pltpu.VMEM(rbf_blocks.shape, bf16),
             pltpu.VMEM(shell_inverse.shape, bf16),
-            pltpu.VMEM((ITERS, 2, chips, shells, breadth), bf16),
+            pltpu.VMEM((ITERS, parts, 2, chips, shells, thin), bf16),
             pltpu.VMEM((ITERS + 1, 2, chips, 1, LANES), f32),
-            state, state, state, state, state,
+            state, state, state, state, state, state,
             history, history, history,
             pltpu.VMEM((ITERS + 1, 1, LANES), f32),
             pltpu.VMEM((ITERS, 1, LANES), f32),
             pltpu.VMEM((2, blocks, half), bf16),
             pltpu.VMEM((2, half, padded), bf16),
             wide, wide, wide, wide,
-            pltpu.VMEM((blocks, 8, nodes), bf16),
-            pltpu.VMEM((ITERS, nodes // LANES, blocks * 8, LANES), f32),
-            pltpu.VMEM((padded, breadth), bf16),
-            pltpu.VMEM((chips, shells, breadth), f32),
-            pltpu.VMEM((chips, shells, breadth), bf16),
-            pltpu.VMEM((chips, shells, breadth), bf16),
-            pltpu.VMEM((far, shells, breadth), bf16),
-            pltpu.VMEM((far, shells, breadth), bf16),
-            dma((5,)), dma,
+            pltpu.VMEM((blocks // 2, 16, nodes), bf16),
+            pltpu.VMEM((ITERS, parts, blocks * 8, LANES), f32),
+            pltpu.VMEM((parts, padded, thin), bf16),
+            pltpu.VMEM((parts, chips, shells, thin), f32),
+            exchange, exchange, exchange, exchange,
+            dma((6,)), dma,
             dma((blocks // LOAD,)),
             dma,
-            dma((far,)), dma((far,)),
-            dma((far + 1,)), dma((far + 1,)),
+            dma((parts, far)), dma((parts, far)),
+            dma((parts, far + 1)), dma((parts, far + 1)),
             dma((2, far + 1, 2)), dma((2, far + 1, 2)),
-            dma, dma,
-            dma((far,)), dma((far,)),
+            dma((parts,)), dma((parts,)),
+            dma((parts, far)), dma((parts, far)),
         ],
         compiler_params=pltpu.CompilerParams(
             collective_id=0, has_side_effects=True, vmem_limit_bytes=VMEM_BYTES

time: 140 us -> 136 us (0.971)
  Pallas kernels: 139 us -> 136 us
    pallas_call x1, Pallas kernels: 137 us -> 134 us  [fused(): pl.pallas_call(functools.partial(kernel, nf, nz, blocks, nodes, shells, 2...]
where the time goes in v3:
time: 136 us
  Pallas kernels  136 us (100%)
    pallas_call x1, Pallas kernels, fused(): pl.pallas_call(functools.partial(kernel, nf, nz, blocks, nodes, shells, 2...  134 us

profile of v3, /device:TPU:0, one launch (start us, length us, event | category | flops | bytes accessed | tf_op | source)
XLA Modules:
  0.0 136.2 jit_solution(12891520577331646073)
XLA Ops:
  0.6 134.0 %coupling.1 = (f32[8,768]{1,0:T(8,128)}, bf16[104,768]{1,0:T(8,128)(2,1)}, f32[6,1,128]{2,1,0:T(1,128)}) custom-call(f32[8,768]{1,0:T(8,128)} %start_hbm.1, s32[1,104]{1,0:T(1,128)} %bitcast.2, s32[1,104]{1,0:T(1,128)} %bitcast.3, bf16[104,768]{1,0:T(8,128)(2,1)} %tr_hbm.1, bf16[104,768]{1,0:T(8,128)(2,1)} %ms_hbm.1, f32[8,768]{1,0:T(8,128)} %robin_hbm.1, ...), custom_call_target="tpu_custom_call" | custom-call | tf_op jit(solution)/shard_map/coupling/pallas_call | solution.py:715
  134.6 1.6 %results.1 = (f32[8,768]{1,0:T(8,128)}, bf16[104,768]{1,0:T(8,128)(2,1)}, f32[6]{0:T(128)}) custom-call(f32[8,768]{1,0:T(8,128)} %get-tuple-element.6.current, bf16[104,768]{1,0:T(8,128)(2,1)} %get-tuple-element.7.load, f32[6,1,128]{2,1,0:T(1,128)} %get-tuple-element.8.norms), custom_call_target="tpu_custom_call" | custom-call | tf_op jit(solution)/shard_map/results/pallas_call | solution.py:767

commit v4 on v3

--- a/solution.py
+++ b/solution.py
@@ -154,9 +154,8 @@
 
 
 CHUNK = 52
-LOAD = 26
+LOAD = 8
 TAIL = 52
-TURN = 4
 LANES = 128
 VMEM_BYTES = 67043328
 MESH = pl.DeviceIdType.MESH
@@ -192,20 +191,28 @@
     nload = blocks // LOAD
     ngroup = blocks // 8
 
+    nb = 2 if nz % 2 == 0 else 1
+    na = nz // nb
+
     def hops(step):
-        ey, ex, ez = step
-        return min(ey, ny - ey) + min(ex, nx - ex) + min(ez, nz - ez)
+        ey, ex, ea, eb = step
+        return ey + ex + ea * nb + eb
 
     steps = sorted(
-        [(ey, ex, ez) for ey in range(ny) for ex in range(nx) for ez in range(nz) if ey + ex + ez],
+        [
+            (ey, ex, ea, eb)
+            for ey in range(ny) for ex in range(nx) for ea in range(na) for eb in range(nb)
+            if ey + ex + ea + eb
+        ],
         key=hops, reverse=True,
     )
     far = len(steps)
 
     def away(step, sign=1):
-        ey, ex, ez = step
+        ey, ex, ea, eb = step
         plane = lax.rem(y + sign * ey + ny, ny) * nx + lax.rem(x + sign * ex + nx, nx)
-        return plane, lax.rem(z + sign * ez + nz, nz)
+        depth = lax.rem(z // nb + sign * ea + na, na) * nb + lax.rem(lax.rem(z, nb) + sign * eb + nb, nb)
+        return plane, depth
 
     targets = [away(s) for s in steps]
     sources = [away(s, -1) for s in steps]
@@ -221,6 +228,8 @@
             device_id=(plane * 2 + unit, depth), device_id_type=MESH,
         )
 
+    first = pltpu.make_async_copy(start_hbm, start_ref, in_sem.at[0])
+    first.start()
     barrier = pltpu.get_barrier_semaphore()
     for plane, depth in targets + [(xy, z)]:
         for unit in (core, other):
@@ -238,9 +247,9 @@
         return pltpu.make_async_copy(inv_hbm, inv, inv_sem)
 
     smalls = [
-        pltpu.make_async_copy(src, dst, in_sem.at[i])
+        pltpu.make_async_copy(src, dst, in_sem.at[i + 1])
         for i, (src, dst) in enumerate((
-            (start_hbm, start_ref), (route_hbm, route_ref), (slot_hbm, slot_ref), (tr_hbm, tr_ref),
+            (route_hbm, route_ref), (slot_hbm, slot_ref), (tr_hbm, tr_ref),
             (ms_hbm, ms_ref), (robin_hbm, robin_ref),
         ))
     ]
@@ -282,7 +291,7 @@
             ag(j, h, k, True).wait_recv()
             ag_pair(j, h, k).start()
 
-    smalls[0].wait()
+    first.wait()
     for h in range(parts):
         xcur[h] = halved(start_ref, h)
     pl.semaphore_wait(barrier, 2 * far + 1)
@@ -301,7 +310,7 @@
         return c
 
     lax.fori_loop(0, ngroup, clear, 0)
-    for copy in smalls[1:]:
+    for copy in smalls:
         copy.wait()
     for h in range(parts):
         robin[h] = halved(robin_ref, h)
@@ -340,13 +349,20 @@
         ids = (lane // group * 2 + unit) * group + lax.rem(lane, group)
         place[side] = jnp.where(ids.astype(f32) == column, 1.0, 0.0).astype(bf16)
 
+    def turn(i, c):
+        rbf_copy(i).wait()
+        for u in range(LOAD):
+            flip[i * LOAD + u] = rbf[i * LOAD + u].T
+        return c
+
+    lax.fori_loop(0, nload, turn, 0)
     lane = lax.broadcasted_iota(jnp.int32, (1, LANES), 1)
 
     def pick(vector, q):
         return jnp.sum(jnp.where(lane == q, vector, 0.0), axis=1, keepdims=True)
 
-    def dot(a, b, dims=((1,), (0,))):
-        return lax.dot_general(a, b, (dims, ((), ())), preferred_element_type=f32)
+    def dot(a, b):
+        return jnp.dot(a, b, preferred_element_type=f32)
 
     def scalar_copies(j, incoming=False):
         copies = []
@@ -443,7 +459,7 @@
     def iteration(j, carry):
         def fetch(h):
             def side(unit):
-                return gath[j, h, unit].astype(f32).reshape(half, thin).astype(bf16)
+                return gath[j, h, unit].reshape(half, thin)
 
             picked = dot(place[0], side(core))
             for k in range(far + 1):
@@ -453,7 +469,7 @@
                 for c in range(3):
                     disp8[h, strided(q, c), :] = picked[q * 8:(q + 1) * 8, thin_of(c)]
 
-        def move(i, size, h, turned):
+        def move(i, size, h):
             cut = slice(h * LANES, (h + 1) * LANES)
             for u in range(0, size, 2):
                 b = i * size + u
@@ -462,11 +478,7 @@
                 left = jnp.concatenate(
                     [jnp.where(upper, both, 0.0), jnp.where(upper, 0.0, both)], axis=1
                 ).astype(bf16)
-                if turned:
-                    shift = dot(left, jnp.concatenate([flip[b, cut, :], flip[b + 1, cut, :]], axis=0))
-                else:
-                    right = jnp.concatenate([rbf[b, :, cut], rbf[b + 1, :, cut]], axis=1)
-                    shift = dot(left, right, ((1,), (1,)))
+                shift = dot(left, jnp.concatenate([flip[b, cut, :], flip[b + 1, cut, :]], axis=0))
                 if h > 0:
                     shift = shift + rows_of(moved.at[j], at)
                 set_rows(moved.at[j], at, shift)
@@ -475,33 +487,16 @@
                     load8[i * (size // 2) + u // 2] = load.astype(bf16)
 
         def forward(h):
-            @pl.when(j == 0)
-            def _():
-                def first(i, c):
-                    if h == 0:
-                        rbf_copy(i).wait()
-
-                        @pl.when(i == nload // 2)
-                        def _():
-                            relay(j, 1)
-
-                    move(i, LOAD, h, False)
-                    return c
-
-                lax.fori_loop(0, nload, first, 0)
-
-            @pl.when(j > 0)
-            def _():
-                def later(i, c):
-                    if h == 0:
-                        @pl.when(i == nchunk // 2)
-                        def _():
-                            relay(j, 1)
-
-                    move(i, CHUNK, h, True)
-                    return c
-
-                lax.fori_loop(0, nchunk, later, 0)
+            def step(i, c):
+                if h == 0:
+                    @pl.when(i == nchunk // 2)
+                    def _():
+                        relay(j, 1)
+
+                move(i, CHUNK, h)
+                return c
+
+            lax.fori_loop(0, nchunk, step, 0)
 
         def backward(h, size):
             cut = slice(h * LANES, (h + 1) * LANES)
@@ -578,12 +573,6 @@
 
         @pl.when(j == 0)
         def _():
-            def turn(i, c):
-                for u in range(TURN):
-                    flip[i * TURN + u] = rbf[i * TURN + u].T
-                return c
-
-            lax.fori_loop(0, blocks // TURN, turn, 0)
             inv_copy().wait()
 
         def forcing(h):

time: 136 us -> 133 us (0.978)
  Pallas kernels: 136 us -> 132 us
    pallas_call x1, Pallas kernels: 134 us -> 131 us  [fused(): pl.pallas_call(functools.partial(kernel, nf, nz, blocks, nodes, shells, 2...]
where the time goes in v4:
time: 133 us
  Pallas kernels  132 us (99%)
    pallas_call x1, Pallas kernels, fused(): pl.pallas_call(functools.partial(kernel, nf, nz, blocks, nodes, shells, 2...  131 us

profile of v4, /device:TPU:0, one launch (start us, length us, event | category | flops | bytes accessed | tf_op | source)
XLA Modules:
  0.0 133.0 jit_solution(17465229230477948895)
XLA Ops:
  0.6 130.7 %coupling.1 = (f32[8,768]{1,0:T(8,128)}, bf16[104,768]{1,0:T(8,128)(2,1)}, f32[6,1,128]{2,1,0:T(1,128)}) custom-call(f32[8,768]{1,0:T(8,128)} %start_hbm.1, s32[1,104]{1,0:T(1,128)} %bitcast.2, s32[1,104]{1,0:T(1,128)} %bitcast.3, bf16[104,768]{1,0:T(8,128)(2,1)} %tr_hbm.1, bf16[104,768]{1,0:T(8,128)(2,1)} %ms_hbm.1, f32[8,768]{1,0:T(8,128)} %robin_hbm.1, ...), custom_call_target="tpu_custom_call" | custom-call | tf_op jit(solution)/shard_map/coupling/pallas_call | solution.py:704
  131.3 1.6 %results.1 = (f32[8,768]{1,0:T(8,128)}, bf16[104,768]{1,0:T(8,128)(2,1)}, f32[6]{0:T(128)}) custom-call(f32[8,768]{1,0:T(8,128)} %get-tuple-element.6.current, bf16[104,768]{1,0:T(8,128)(2,1)} %get-tuple-element.7.load, f32[6,1,128]{2,1,0:T(1,128)} %get-tuple-element.8.norms), custom_call_target="tpu_custom_call" | custom-call | tf_op jit(solution)/shard_map/results/pallas_call | solution.py:756

commit v5 on v4

--- a/solution.py
+++ b/solution.py
@@ -153,9 +153,9 @@
     return (current, last_load, jnp.stack(norms))
 
 
-CHUNK = 52
 LOAD = 8
-TAIL = 52
+FIRST = 0
+LAST = 52
 LANES = 128
 VMEM_BYTES = 67043328
 MESH = pl.DeviceIdType.MESH
@@ -187,7 +187,6 @@
     other = 1 - core
     xy = f // 2
     x, y = lax.rem(xy, nx), xy // nx
-    nchunk = blocks // CHUNK
     nload = blocks // LOAD
     ngroup = blocks // 8
 
@@ -469,11 +468,10 @@
                 for c in range(3):
                     disp8[h, strided(q, c), :] = picked[q * 8:(q + 1) * 8, thin_of(c)]
 
-        def move(i, size, h):
+        def move(begin, end, h):
             cut = slice(h * LANES, (h + 1) * LANES)
-            for u in range(0, size, 2):
-                b = i * size + u
-                at = pl.ds(pl.multiple_of(b * 8, 16), 16)
+            for b in range(begin, end, 2):
+                at = pl.ds(b * 8, 16)
                 both = disp8[h, at, :]
                 left = jnp.concatenate(
                     [jnp.where(upper, both, 0.0), jnp.where(upper, 0.0, both)], axis=1
@@ -484,39 +482,15 @@
                 set_rows(moved.at[j], at, shift)
                 if h == parts - 1:
                     load = rows_of(tr8, at) - rows_of(ms8, at) * shift
-                    load8[i * (size // 2) + u // 2] = load.astype(bf16)
-
-        def forward(h):
-            def step(i, c):
-                if h == 0:
-                    @pl.when(i == nchunk // 2)
-                    def _():
-                        relay(j, 1)
-
-                move(i, CHUNK, h)
-                return c
-
-            lax.fori_loop(0, nchunk, step, 0)
-
-        def backward(h, size):
+                    load8[b // 2] = load.astype(bf16)
+
+        def back(begin, end, h):
             cut = slice(h * LANES, (h + 1) * LANES)
-
-            def back(i, c):
-                if h > 0:
-                    @pl.when(i == blocks // size - 1)
-                    def _():
-                        spread_out(h - 1)
-
-                for u in range(0, size, 2):
-                    b = i * size + u
-                    at = pl.multiple_of(b * 8, 16)
-                    right = jnp.concatenate([rbf[b, :, cut], rbf[b + 1, :, cut]], axis=1)
-                    both = dot(load8[i * (size // 2) + u // 2], right)
-                    map8[h, pl.ds(at, 8), :] = both[0:8, 0:LANES]
-                    map8[h, pl.ds(at + 8, 8), :] = both[8:16, LANES:2 * LANES]
-                return c
-
-            lax.fori_loop(0, blocks // size, back, 0)
+            for b in range(begin, end, 2):
+                right = jnp.concatenate([rbf[b, :, cut], rbf[b + 1, :, cut]], axis=1)
+                both = dot(load8[b // 2], right)
+                map8[h, pl.ds(b * 8, 8), :] = both[0:8, 0:LANES]
+                map8[h, pl.ds(b * 8 + 8, 8), :] = both[8:16, LANES:2 * LANES]
 
         def copy_a(h):
             return remote(send_a.at[h], recv_a.at[h], ra_s.at[h], ra_r.at[h], xy, other, z)
@@ -547,12 +521,16 @@
 
         relay(j, 0)
         fetch(0)
-        forward(0)
+        move(0, FIRST, 0)
+        relay(j, 1)
+        move(FIRST, blocks, 0)
         fetch(1)
-        forward(1)
-        backward(0, CHUNK)
+        move(0, blocks, 1)
+        back(0, blocks, 0)
         gather_up(0)
-        backward(1, TAIL)
+        back(0, LAST, 1)
+        spread_out(0)
+        back(LAST, blocks, 1)
         gather_up(1)
         spread_out(1)
 

time: 133 us -> 127 us (0.955)
  Pallas kernels: 132 us -> 127 us
    pallas_call x1, Pallas kernels: 131 us -> 125 us  [fused(): pl.pallas_call(functools.partial(kernel, nf, nz, blocks, nodes, shells, 2...]
where the time goes in v5:
time: 127 us
  Pallas kernels  127 us (100%)
    pallas_call x1, Pallas kernels, fused(): pl.pallas_call(functools.partial(kernel, nf, nz, blocks, nodes, shells, 2...  125 us

profile of v5, /device:TPU:0, one launch (start us, length us, event | category | flops | bytes accessed | tf_op | source)
XLA Modules:
  0.0 127.2 jit_solution(10207086652873691057)
XLA Ops:
  0.6 124.9 %coupling.1 = (f32[8,768]{1,0:T(8,128)}, bf16[104,768]{1,0:T(8,128)(2,1)}, f32[6,1,128]{2,1,0:T(1,128)}) custom-call(f32[8,768]{1,0:T(8,128)} %start_hbm.1, s32[1,104]{1,0:T(1,128)} %bitcast.2, s32[1,104]{1,0:T(1,128)} %bitcast.3, bf16[104,768]{1,0:T(8,128)(2,1)} %tr_hbm.1, bf16[104,768]{1,0:T(8,128)(2,1)} %ms_hbm.1, f32[8,768]{1,0:T(8,128)} %robin_hbm.1, ...), custom_call_target="tpu_custom_call" | custom-call | tf_op jit(solution)/shard_map/coupling/pallas_call | solution.py:682
  125.5 1.6 %results.1 = (f32[8,768]{1,0:T(8,128)}, bf16[104,768]{1,0:T(8,128)(2,1)}, f32[6]{0:T(128)}) custom-call(f32[8,768]{1,0:T(8,128)} %get-tuple-element.6.current, bf16[104,768]{1,0:T(8,128)(2,1)} %get-tuple-element.7.load, f32[6,1,128]{2,1,0:T(1,128)} %get-tuple-element.8.norms), custom_call_target="tpu_custom_call" | custom-call | tf_op jit(solution)/shard_map/results/pallas_call | solution.py:734
